TPU v7x, 8 devices: a whole 2x2x1 slice. The times are simulated.
8 devices in a mesh: ens: 2 (over z, y), feat: 4 (over x, core).
Axes of the slice: x: 2, y: 2, z: 1, core: 2. Of those that a mesh axis runs over, the one named last changes fastest.
Arguments:
- particles: float32 [4, 512, 16384], P('ens', None, 'feat'), parts along dimension 0
- target_mean: float32 [4, 16384], P('ens', 'feat'), parts along dimension 0
- precision: float32 [32768], P(('ens', 'feat')), parts along dimension 0
- low_factor: bfloat16 [32768, 128], P(('ens', 'feat')), parts along dimension 0
Outputs:
- output: float32 [4, 512, 16384], P('ens', None, 'feat'), parts along dimension 0
There are 2 independent parts. A program takes and returns all parts, laid end to end along the dimension named above; each array names one.
All inputs are finite; a program needn't handle non-finite values.
Results may differ from a plain program's by a relative error of at most 0.001.
Values are sent between devices in bfloat16 or wider.
A program may use at most 1 GiB of HBM per device.

v0:
```python
import jax
import jax.numpy as jnp
from jax import lax
from jax.sharding import PartitionSpec as P

NUM_STEPS = 3


def solution(mesh):
    feat_count = mesh.shape["feat"]
    data_spec = P("ens", None, "feat")
    mean_spec = P("ens", "feat")
    prec_spec = P(("ens", "feat"))
    factor_spec = P(("ens", "feat"), None)

    def local_steps(particles, target_mean, precision, low_factor):
        num_part = particles.shape[1]
        total_feat = particles.shape[2] * feat_count
        bandwidth = 2.0 * total_feat
        step_size = 0.25 * total_feat
        mean_rows = target_mean[:, None, :]
        theta = particles
        for step_index in range(NUM_STEPS):
            centered = theta - mean_rows
            theta_bf = theta.astype(jnp.bfloat16)
            proj_part = jnp.einsum("end,dr->enr", centered.astype(jnp.bfloat16), low_factor, preferred_element_type=jnp.float32)
            gram_part = jnp.einsum("end,emd->enm", theta_bf, theta_bf, preferred_element_type=jnp.float32)
            project, gram_mat = lax.psum((proj_part, gram_part), "feat")
            gram_diag = jnp.diagonal(gram_mat, axis1=1, axis2=2)
            sq_dist = jnp.maximum(gram_diag[:, :, None] + gram_diag[:, None, :] - 2.0 * gram_mat, 0.0)
            kernel = jnp.exp(-sq_dist / bandwidth)
            low_term = jnp.einsum("enr,dr->end", project.astype(jnp.bfloat16), low_factor, preferred_element_type=jnp.float32)
            grad_log = -(centered * precision + low_term)
            mixed = (grad_log - (2.0 / bandwidth) * theta).astype(jnp.bfloat16)
            drive = jnp.einsum("enm,emd->end", kernel.astype(jnp.bfloat16), mixed, preferred_element_type=jnp.float32)
            row_sum = jnp.sum(kernel, axis=2, keepdims=True)
            theta = theta + step_size * ((drive + (2.0 / bandwidth) * row_sum * theta) / num_part)
        return theta

    return jax.shard_map(local_steps, mesh=mesh, in_specs=(data_spec, mean_spec, prec_spec, factor_spec), out_specs=data_spec, check_vma=False)
```

profile of v0, /device:TPU:0, one launch (start us, length us, event | category | flops | bytes accessed | tf_op | source)
XLA Modules:
  0.0 481.1 jit_solution(15138404884217842823)
XLA Ops:
  6.5 14.0 %fusion.10 = f32[2,512,512]{2,1,0:T(8,128)} fusion(f32[2,512,4096]{2,1,0:T(8,128)} %param.4), kind=kOutput, calls=%fused_computation.22 | convolution fusion | flops 4299161600 | bytes 18874368 | tf_op jit(solution)/shard_map/end,emd->enm/dot_general | solution.py:27
  20.5 0.0 all-reduce.9.cloned.1.call-start
  20.6 8.1 %fusion = f32[2,512,128]{2,1,0:T(8,128)S(1)} fusion(f32[2,512,4096]{2,1,0:T(8,128)} %param.4, f32[2,4096]{1,0:T(2,128)S(1)} %copy-done.4, bf16[4096,128]{1,0:T(8,128)(2,1)S(1)} %copy-done), kind=kOutput, calls=%fused_computation.12 | convolution fusion | flops 1082130432 | bytes 18382848 | tf_op jit(solution)/shard_map/end,dr->enr/dot_general | solution.py:26
  28.8 25.2 %all-reduce.12 = bf16[2,512,128]{2,1,0:T(8,128)(2,1)S(1)} all-reduce(f32[2,512,128]{2,1,0:T(8,128)S(1)} %fusion), channel_id=1, replica_groups=mesh['ens'=2,'feat'=4] {'feat'}, use_global_device_ids=true, to_apply=%region_1.0 | all-reduce | flops 131072 | bytes 786432 | tf_op jit(solution)/shard_map/psum | solution.py:28
  54.0 9.7 %subtract_convert_fusion.2 = bf16[2,512,4096]{2,1,0:T(8,128)(2,1)} fusion(f32[2,512,4096]{2,1,0:T(8,128)} %param.4, f32[4096]{0:T(1024)S(1)} %copy-done.5, f32[2,4096]{1,0:T(2,128)S(1)} %copy-done.4, bf16[4096,128]{1,0:T(8,128)(2,1)S(1)} %copy-done, bf16[2,512,128]{2,1,0:T(8,128)(2,1)S(1)} %all-reduce.12), kind=kOutput, calls=%fused_computation.8 | convolution fusion | flops 1103101952 | bytes 26525696 | tf_op jit(solution)/shard_map/enr,dr->end/dot_general | solution.py:32
  63.7 12.0 %all-reduce.7.cloned.1.call-done = f32[2,512,512]{2,1,0:T(8,128)} async-done(((f32[2,512,512]{2,1,0:T(8,128)}), f32[2,512,512]{2,1,0:T(8,128)}) %all-reduce.7.cloned.1.call-update) | async-done | bytes 2097168 | tf_op jit(solution)/shard_map/psum | solution.py:28
  75.8 60.2 %copy.14 = f32[2,512,512]{0,2,1:T(8,128)} copy(f32[2,512,512]{2,1,0:T(8,128)} %all-reduce.7.cloned.1.call-done) | data formatting | bytes 4194304 | tf_op jit(solution)/shard_map/psum | solution.py:28
  136.0 5.5 %gather_fusion = f32[512,2]{1,0:T(8,128)S(1)} fusion(f32[2,512,512]{0,2,1:T(8,128)} %copy.14, s32[512]{0:T(512)S(1)} %bitcast.23), kind=kCustom, calls=%fused_computation | custom fusion | bytes 12288 | tf_op jit(solution)/shard_map/jit(diagonal)/gather | solution.py:29
  141.5 0.1 copy.15
  141.6 0.8 fusion.12
  142.4 15.3 %multiply_add_fusion.2 = f32[2,512,4096]{2,1,0:T(8,128)} fusion(f32[2,512,4096]{2,1,0:T(8,128)} %param.4, f32[2,512]{1,0:T(2,128)S(1)} %broadcast_multiply_fusion.2, bf16[2,512,4096]{2,1,0:T(8,128)(2,1)} %subtract_convert_fusion.2, f32[2,512,512]{2,1,0:T(8,128)S(1)} %copy-done.1, f32[2,512]{1,0:T(2,128)S(1)} %copy.15), kind=kOutput, calls=%fused_computation.7 | convolution fusion | flops 4315414528 | bytes 44048384 | tf_op jit(solution)/shard_map/enm,emd->end/dot_general | solution.py:35
  157.8 13.9 %fusion.5 = f32[2,512,512]{2,1,0:T(8,128)} fusion(f32[2,512,4096]{2,1,0:T(8,128)} %multiply_add_fusion.2), kind=kOutput, calls=%fused_computation.17 | convolution fusion | flops 4299161600 | bytes 18874368 | tf_op jit(solution)/shard_map/end,emd->enm/dot_general | solution.py:27
  171.7 8.1 %fusion.1 = f32[2,512,128]{2,1,0:T(8,128)S(1)} fusion(f32[2,512,4096]{2,1,0:T(8,128)} %multiply_add_fusion.2, f32[2,4096]{1,0:T(2,128)S(1)} %copy-done.4, bf16[4096,128]{1,0:T(8,128)(2,1)S(1)} %copy-done), kind=kOutput, calls=%fused_computation.13 | convolution fusion | flops 1082130432 | bytes 18382848 | tf_op jit(solution)/shard_map/end,dr->enr/dot_general | solution.py:26
  179.8 0.0 all-reduce.11.cloned.1.call-start
  179.9 25.6 %all-reduce.13 = bf16[2,512,128]{2,1,0:T(8,128)(2,1)S(1)} all-reduce(f32[2,512,128]{2,1,0:T(8,128)S(1)} %fusion.1), channel_id=1, replica_groups=mesh['ens'=2,'feat'=4] {'feat'}, use_global_device_ids=true, to_apply=%region_4.5 | all-reduce | flops 131072 | bytes 786432 | tf_op jit(solution)/shard_map/psum | solution.py:28
  205.5 9.8 %subtract_convert_fusion.1 = bf16[2,512,4096]{2,1,0:T(8,128)(2,1)} fusion(f32[2,512,4096]{2,1,0:T(8,128)} %multiply_add_fusion.2, f32[4096]{0:T(1024)S(1)} %copy-done.5, f32[2,4096]{1,0:T(2,128)S(1)} %copy-done.4, bf16[4096,128]{1,0:T(8,128)(2,1)S(1)} %copy-done, bf16[2,512,128]{2,1,0:T(8,128)(2,1)S(1)} %all-reduce.13), kind=kOutput, calls=%fused_computation.6 | convolution fusion | flops 1103101952 | bytes 26525696 | tf_op jit(solution)/shard_map/enr,dr->end/dot_general | solution.py:32
  215.2 19.0 %all-reduce.9.cloned.1.call-done = f32[2,512,512]{2,1,0:T(8,128)} async-done(((f32[2,512,512]{2,1,0:T(8,128)}), f32[2,512,512]{2,1,0:T(8,128)}) %all-reduce.9.cloned.1.call-update) | async-done | bytes 2097168 | tf_op jit(solution)/shard_map/psum | solution.py:28
  234.2 60.2 %copy.17 = f32[2,512,512]{0,2,1:T(8,128)} copy(f32[2,512,512]{2,1,0:T(8,128)} %all-reduce.9.cloned.1.call-done) | data formatting | bytes 4194304 | tf_op jit(solution)/shard_map/psum | solution.py:28
  294.4 5.5 %gather_fusion.1 = f32[512,2]{1,0:T(8,128)S(1)} fusion(f32[2,512,512]{0,2,1:T(8,128)} %copy.17, s32[512]{0:T(512)S(1)} %bitcast.24), kind=kCustom, calls=%fused_computation.1 | custom fusion | bytes 12288 | tf_op jit(solution)/shard_map/jit(diagonal)/gather | solution.py:29
  299.9 0.1 copy.18
  300.0 0.8 fusion.14
  300.8 15.4 %multiply_add_fusion.1 = f32[2,512,4096]{2,1,0:T(8,128)} fusion(f32[2,512,4096]{2,1,0:T(8,128)} %multiply_add_fusion.2, f32[2,512]{1,0:T(2,128)S(1)} %broadcast_multiply_fusion.1, bf16[2,512,4096]{2,1,0:T(8,128)(2,1)} %subtract_convert_fusion.1, f32[2,512,512]{2,1,0:T(8,128)S(1)} %copy-done.2, f32[2,512]{1,0:T(2,128)S(1)} %copy.18), kind=kOutput, calls=%fused_computation.5 | convolution fusion | flops 4315414528 | bytes 44048384 | tf_op jit(solution)/shard_map/enm,emd->end/dot_general | solution.py:35
  316.2 13.9 %fusion.3 = f32[2,512,512]{2,1,0:T(8,128)} fusion(f32[2,512,4096]{2,1,0:T(8,128)} %multiply_add_fusion.1), kind=kOutput, calls=%fused_computation.15 | convolution fusion | flops 4299161600 | bytes 18874368 | tf_op jit(solution)/shard_map/end,emd->enm/dot_general | solution.py:27
  330.1 8.1 %fusion.2 = f32[2,512,128]{2,1,0:T(8,128)S(1)} fusion(f32[2,512,4096]{2,1,0:T(8,128)} %multiply_add_fusion.1, f32[2,4096]{1,0:T(2,128)S(1)} %copy-done.4, bf16[4096,128]{1,0:T(8,128)(2,1)S(1)} %copy-done), kind=kOutput, calls=%fused_computation.14 | convolution fusion | flops 1082130432 | bytes 18382848 | tf_op jit(solution)/shard_map/end,dr->enr/dot_general | solution.py:26
  338.3 25.6 %all-reduce.14 = bf16[2,512,128]{2,1,0:T(8,128)(2,1)S(1)} all-reduce(f32[2,512,128]{2,1,0:T(8,128)S(1)} %fusion.2), channel_id=1, replica_groups=mesh['ens'=2,'feat'=4] {'feat'}, use_global_device_ids=true, to_apply=%region_7.8 | all-reduce | flops 131072 | bytes 786432 | tf_op jit(solution)/shard_map/psum | solution.py:28
  363.9 9.7 %subtract_convert_fusion = bf16[2,512,4096]{2,1,0:T(8,128)(2,1)} fusion(f32[2,512,4096]{2,1,0:T(8,128)} %multiply_add_fusion.1, f32[4096]{0:T(1024)S(1)} %copy-done.5, f32[2,4096]{1,0:T(2,128)S(1)} %copy-done.4, bf16[4096,128]{1,0:T(8,128)(2,1)S(1)} %copy-done, bf16[2,512,128]{2,1,0:T(8,128)(2,1)S(1)} %all-reduce.14), kind=kOutput, calls=%fused_computation.4 | convolution fusion | flops 1103101952 | bytes 26525696 | tf_op jit(solution)/shard_map/enr,dr->end/dot_general | solution.py:32
  373.6 18.9 %all-reduce.11.cloned.1.call-done = f32[2,512,512]{2,1,0:T(8,128)} async-done(((f32[2,512,512]{2,1,0:T(8,128)}), f32[2,512,512]{2,1,0:T(8,128)}) %all-reduce.11.cloned.1.call-update) | async-done | bytes 2097168 | tf_op jit(solution)/shard_map/psum | solution.py:28
  392.6 60.2 %copy.20 = f32[2,512,512]{0,2,1:T(8,128)} copy(f32[2,512,512]{2,1,0:T(8,128)} %all-reduce.11.cloned.1.call-done) | data formatting | bytes 4194304 | tf_op jit(solution)/shard_map/psum | solution.py:28
  452.8 5.5 %gather_fusion.2 = f32[512,2]{1,0:T(8,128)S(1)} fusion(f32[2,512,512]{0,2,1:T(8,128)} %copy.20, s32[512]{0:T(512)S(1)} %bitcast.25), kind=kCustom, calls=%fused_computation.2 | custom fusion | bytes 12288 | tf_op jit(solution)/shard_map/jit(diagonal)/gather | solution.py:29
  458.3 0.1 copy.21
  458.4 0.8 fusion.16
  459.2 15.3 %multiply_add_fusion = f32[2,512,4096]{2,1,0:T(8,128)} fusion(f32[2,512,4096]{2,1,0:T(8,128)} %multiply_add_fusion.1, f32[2,512]{1,0:T(2,128)S(1)} %broadcast_multiply_fusion, bf16[2,512,4096]{2,1,0:T(8,128)(2,1)} %subtract_convert_fusion, f32[2,512,512]{2,1,0:T(8,128)S(1)} %copy-done.3, f32[2,512]{1,0:T(2,128)S(1)} %copy.21), kind=kOutput, calls=%fused_computation.3 | convolution fusion | flops 4315414528 | bytes 44048384 | tf_op jit(solution)/shard_map/enm,emd->end/dot_general | solution.py:35
  (20 shorter events, 0.1 us)
Async XLA Ops:
  6.5 14.1 %copy-start = (bf16[4096,128]{1,0:T(8,128)(2,1)S(1)}, bf16[4096,128]{1,0:T(8,128)(2,1)}, u32[]{:S(2)}) copy-start(bf16[4096,128]{1,0:T(8,128)(2,1)} %param.7) | copy-start | bytes 3145732
  6.5 14.1 %copy-start.4 = (f32[2,4096]{1,0:T(2,128)S(1)}, f32[2,4096]{1,0:T(2,128)}, u32[]{:S(2)}) copy-start(f32[2,4096]{1,0:T(2,128)} %param.5) | copy-start | bytes 98308
  6.5 69.2 %all-reduce.7.cloned.1.call-start = ((), (), s32[]{:S(2)}) async-start(), calls=%async_computation | async-start | bytes 4194304 | tf_op jit(solution)/shard_map/psum | solution.py:28
  20.5 213.6 %all-reduce.9.cloned.1.call-start = ((), (), s32[]{:S(2)}) async-start(), calls=%async_computation.1 | async-start | bytes 4194304 | tf_op jit(solution)/shard_map/psum | solution.py:28
  20.6 33.3 %copy-start.5 = (f32[4096]{0:T(1024)S(1)}, f32[4096]{0:T(1024)}, u32[]{:S(2)}) copy-start(f32[4096]{0:T(1024)} %param.6) | copy-start | bytes 49156
  75.8 65.9 %copy-start.1 = (f32[2,512,512]{2,1,0:T(8,128)S(1)}, f32[2,512,512]{2,1,0:T(8,128)}, u32[]{:S(2)}) copy-start(f32[2,512,512]{2,1,0:T(8,128)} %all-reduce.7.cloned.1.call-done) | copy-start | bytes 6291460
  179.8 212.7 %all-reduce.11.cloned.1.call-start = ((), (), s32[]{:S(2)}) async-start(), calls=%async_computation.2 | async-start | bytes 4194304 | tf_op jit(solution)/shard_map/psum | solution.py:28
  234.2 65.9 %copy-start.2 = (f32[2,512,512]{2,1,0:T(8,128)S(1)}, f32[2,512,512]{2,1,0:T(8,128)}, u32[]{:S(2)}) copy-start(f32[2,512,512]{2,1,0:T(8,128)} %all-reduce.9.cloned.1.call-done) | copy-start | bytes 6291460
  392.6 65.9 %copy-start.3 = (f32[2,512,512]{2,1,0:T(8,128)S(1)}, f32[2,512,512]{2,1,0:T(8,128)}, u32[]{:S(2)}) copy-start(f32[2,512,512]{2,1,0:T(8,128)} %all-reduce.11.cloned.1.call-done) | copy-start | bytes 6291460
Sparse Core Ops, SparseCore 0:
  20.7 55.0 all-reduce.6
  179.9 54.1 all-reduce.8
  338.4 54.1 all-reduce.10
where the time goes:
time: 487 us; the launch traced here: 481 us
  local copies, waits for them, and re-layouts  198 us (41%)
  matrix products  141 us (29%)
  blocking collectives  76.4 us (16%)
  waiting for transfers between devices  50 us (10%)
  between operations  13.2 us (3%)
    psum x3, local copies, waits for them, and re-layouts, local_steps(): project, gram_mat = lax.psum((proj_part, gram_part), 'feat')  181 us
    psum x3, blocking collectives, local_steps(): project, gram_mat = lax.psum((proj_part, gram_part), 'feat')  76.4 us
    psum x3, waiting for transfers between devices, local_steps(): project, gram_mat = lax.psum((proj_part, gram_part), 'feat')  50 us
    dot_general x3, matrix products, local_steps(): jnp.einsum('enm,emd->end', kernel.astype(jnp.bfloat16), mixed, preferred_...  46 us
    dot_general x3, matrix products, local_steps(): jnp.einsum('end,emd->enm', theta_bf, theta_bf, preferred_element_type=jnp...  41.8 us
    dot_general x3, matrix products, local_steps(): jnp.einsum('enr,dr->end', project.astype(jnp.bfloat16), low_factor, prefe...  29.2 us
    dot_general x3, matrix products, local_steps(): jnp.einsum('end,dr->enr', centered.astype(jnp.bfloat16), low_factor, pref...  24.3 us
    gather x6, local copies, waits for them, and re-layouts, local_steps(): gram_diag = jnp.diagonal(gram_mat, axis1=1, axis2=2)  16.9 us
  transfers between devices with their start and end apart: 3, of which 3 were waited for; matrix products, arithmetic and copies ran while one was open for 8% of the time, Pallas kernels for 0%

commit v1 on v0

v1 whole, which is shorter than its diff:
```python
import jax
import jax.numpy as jnp
from jax import lax
from jax.experimental import pallas as pl
from jax.experimental.pallas import tpu as pltpu
from jax.sharding import PartitionSpec as P

NUM_STEPS = 3
BLK = 128
TILE = 512
F32 = jnp.float32
BF16 = jnp.bfloat16
TRANS_B = (((1,), (1,)), ((), ()))

SEM_CORE, SEM_CHIP, SEM_GATHER, SEM_OWN, SEM_FWD = range(5)
NUM_KINDS = 3
NUM_SEMS = 5 * NUM_KINDS


def build_kernel(num_part, num_local, total_feat):
    nblk = num_part // BLK
    num_tiles = num_local // TILE
    bandwidth = 2.0 * total_feat
    step_size = 0.25 * total_feat
    two_h = 2.0 / bandwidth
    gain = step_size / num_part
    grow = 2 * BLK + BLK // 2

    def kernel(th_hbm, mu_ref, lam_ref, u_ref, out_hbm,
               theta, tb, kfull, qacc, scol,
               pq, pg, pd, rq, rg, rd, sq, sg, sd, xq, xg, xd, dfull, gsum,
               qall, kall, sall,
               in_sem, out_sem, send_sem, recv_sem):
        feat = lax.axis_index("feat")
        chip = feat // 2
        core = feat % 2
        own = 2 * core + chip
        peer_core = {"feat": 2 * chip + (1 - core)}
        peer_chip = {"feat": 2 * (1 - chip) + core}

        barrier = pltpu.get_barrier_semaphore()
        for peer in (peer_core, peer_chip):
            pl.semaphore_signal(barrier, inc=1, device_id=peer, device_id_type=pl.DeviceIdType.MESH)
        pl.semaphore_wait(barrier, 2)

        def rcopy(src, dst, e, group, kind, peer):
            idx = group * NUM_KINDS + kind
            return pltpu.make_async_remote_copy(
                src_ref=src, dst_ref=dst, send_sem=send_sem.at[e, idx], recv_sem=recv_sem.at[e, idx],
                device_id=peer, device_id_type=pl.DeviceIdType.MESH)

        def tile_ds(t):
            return pl.ds(pl.multiple_of(t * TILE, TILE), TILE)

        def in_copy(e, t):
            return pltpu.make_async_copy(th_hbm.at[e, :, tile_ds(t)], theta.at[e, :, tile_ds(t)], in_sem.at[e, t])

        def out_copy(e, t):
            return pltpu.make_async_copy(theta.at[e, :, tile_ds(t)], out_hbm.at[e, :, tile_ds(t)], out_sem.at[e, t])

        def core_q(e):
            return rcopy(pq.at[e, pl.ds(2 * (1 - core), 2)], rq.at[e], e, SEM_CORE, 0, peer_core)

        def core_g(e):
            return rcopy(pg.at[e, pl.ds(2 * (1 - core), 2)], rg.at[e], e, SEM_CORE, 1, peer_core)

        def core_d(e):
            return rcopy(pd.at[e], rd.at[e], e, SEM_CORE, 2, peer_core)

        def chip_q(e):
            return rcopy(sq.at[e, 1 - chip], xq.at[e], e, SEM_CHIP, 0, peer_chip)

        def chip_g(e):
            return rcopy(sg.at[e, 1 - chip], xg.at[e], e, SEM_CHIP, 1, peer_chip)

        def chip_d(e):
            return rcopy(sd.at[e], xd.at[e], e, SEM_CHIP, 2, peer_chip)

        def gather(e, slot, group, kind, peer):
            buf = (qall, kall, sall)[kind]
            if kind == 0:
                ref = buf.at[e, pl.ds(pl.multiple_of(slot * BLK, BLK), BLK)]
            else:
                ref = buf.at[e, slot]
            return rcopy(ref, ref, e, group, kind, peer)

        def to_chip(e, kind):
            return gather(e, own, SEM_GATHER, kind, peer_chip)

        def to_core(e, kind):
            return gather(e, own, SEM_OWN, kind, peer_core)

        def forward(e, kind):
            return gather(e, 2 * core + (1 - chip), SEM_FWD, kind, peer_core)

        def stage2_q(e):
            core_q(e).wait()
            for c in range(2):
                sq[e, c] = pq[e, 2 * core + c] + rq[e, c]
            chip_q(e).start()

        def stage2_g(e):
            core_g(e).wait()
            core_d(e).wait()
            sd[e] = pd[e] + rd[e]
            chip_d(e).start()
            for c in range(2):
                sg[e, c] = pg[e, 2 * core + c] + rg[e, c]
            chip_g(e).start()

        def stage3_q(e):
            chip_q(e).wait()
            full = sq[e, chip] + xq[e]
            qall[e, pl.ds(pl.multiple_of(own * BLK, BLK), BLK), :] = full.astype(BF16)
            to_chip(e, 0).start()
            to_core(e, 0).start()

        def stage3_g(e):
            chip_d(e).wait()
            chip_g(e).wait()
            dfull[...] = sd[e] + xd[e]
            gsum[...] = sg[e, chip] + xg[e]
            sall[e, own] = jnp.zeros((8, BLK), F32)
            wrap = own // 3
            half = own // 2
            parts = (
                (0, BLK, own, own, 0),
                (BLK, BLK, own - 3 * wrap, own + 1 - wrap, 0),
                (2 * BLK, BLK // 2, own % 2, own % 2 + 2, half * (BLK // 2)),
            )
            for index, (start, size, row_blk, col_blk, row_off) in enumerate(parts):
                row_id = lax.broadcasted_iota(jnp.int32, (size, BLK), 0) + row_off
                col_id = lax.broadcasted_iota(jnp.int32, (size, BLK), 1)
                eye = row_id == col_id
                diag_col = jnp.sum(jnp.where(eye, dfull[pl.ds(row_blk, 1), :], 0.0), axis=1, keepdims=True)
                diag_row = dfull[pl.ds(col_blk, 1), :]
                dist = jnp.maximum(diag_col + diag_row - 2.0 * gsum[start:start + size, :], 0.0)
                kern = jnp.exp(-dist / bandwidth)
                kall[e, own, start:start + size, :] = kern.astype(BF16)
                sall[e, own, pl.ds(col_blk, 1), :] += jnp.sum(kern, axis=0, keepdims=True)
                if index > 0:
                    row_sum = jnp.sum(kern, axis=1, keepdims=True)
                    sall[e, own, pl.ds(row_blk, 1), :] += jnp.sum(jnp.where(eye, row_sum, 0.0), axis=0, keepdims=True)
            for kind in (1, 2):
                to_chip(e, kind).start()
                to_core(e, kind).start()

        def stage4(e, kinds):
            for kind in kinds:
                to_chip(e, kind).wait()
                forward(e, kind).start()

        def stage5(e):
            for kind in range(NUM_KINDS):
                to_core(e, kind).wait()
                forward(e, kind).wait()
            half = BLK // 2

            def put(i, j, rows, block):
                r0 = i * BLK + rows
                n = block.shape[0]
                kfull[r0:r0 + n, j * BLK:(j + 1) * BLK] = block

            def put_pair(i, j, block):
                put(i, j, 0, block)
                put(j, i, 0, block.astype(F32).T.astype(BF16))

            for i in range(nblk):
                put(i, i, 0, kall[e, i, 0:BLK, :])
            for i, j, o in ((0, 1, 0), (1, 2, 1), (2, 3, 2), (0, 3, 3)):
                put_pair(i, j, kall[e, o, BLK:2 * BLK, :])
            for i in range(2):
                lo = kall[e, i, 2 * BLK:2 * BLK + half, :]
                hi = kall[e, i + 2, 2 * BLK:2 * BLK + half, :]
                put_pair(i, i + 2, jnp.concatenate([lo, hi], axis=0))
            srow = sall[e, 0] + sall[e, 1] + sall[e, 2] + sall[e, 3]
            eye = (lax.broadcasted_iota(jnp.int32, (BLK, BLK), 0) == lax.broadcasted_iota(jnp.int32, (BLK, BLK), 1))
            for i in range(nblk):
                col = jnp.sum(jnp.where(eye, srow[i:i + 1, :], 0.0), axis=1, keepdims=True)
                scol[i * BLK:(i + 1) * BLK, :] = jnp.broadcast_to(col, (BLK, BLK)) * two_h

        def project(e, t, value):
            ds = tile_ds(t)
            tb[:, ds] = value.astype(BF16)
            xb = (value - mu_ref[e, :, ds]).astype(BF16)
            part = jnp.dot(xb, u_ref[ds, :], preferred_element_type=F32)

            @pl.when(t == 0)
            def _():
                qacc[...] = part

            @pl.when(t > 0)
            def _():
                qacc[...] += part

        def update(e, t):
            ds = tile_ds(t)
            value = theta[e, :, ds]
            low = lax.dot_general(qall[e], u_ref[ds, :], TRANS_B, preferred_element_type=F32)
            centered = value - mu_ref[e, :, ds]
            grad = -(centered * lam_ref[:, ds] + low)
            mixed = (grad - two_h * value).astype(BF16)
            drive = jnp.dot(kfull[...], mixed, preferred_element_type=F32)
            new = value + gain * (drive + scol[:, 0:1] * value)
            theta[e, :, ds] = new
            return new

        def send_q(e):
            for i in range(nblk):
                pq[e, i] = qacc[i * BLK:(i + 1) * BLK, :]
            core_q(e).start()

        def gram(e):
            half = BLK // 2
            two = 2 * BLK

            def place(i, j, block):
                if i == j:
                    pg[e, i, 0:BLK, :] = block
                    eye = (lax.broadcasted_iota(jnp.int32, (BLK, BLK), 0) == lax.broadcasted_iota(jnp.int32, (BLK, BLK), 1))
                    pd[e, i:i + 1, :] = jnp.sum(jnp.where(eye, block, 0.0), axis=0, keepdims=True)
                elif j == i + 2:
                    pg[e, i, two:two + half, :] = block[0:half]
                    pg[e, i + 2, two:two + half, :] = block[half:BLK]
                else:
                    pg[e, 3 if (i, j) == (0, 3) else i, BLK:two, :] = block

            right = lax.dot_general(tb[...], tb[two:2 * two, :], TRANS_B, preferred_element_type=F32)
            for i in range(nblk):
                for j in (2, 3):
                    if i <= j:
                        place(i, j, right[i * BLK:(i + 1) * BLK, (j - 2) * BLK:(j - 1) * BLK])
            left = lax.dot_general(tb[0:two, :], tb[0:two, :], TRANS_B, preferred_element_type=F32)
            for i in range(2):
                for j in range(i, 2):
                    place(i, j, left[i * BLK:(i + 1) * BLK, j * BLK:(j + 1) * BLK])
            core_g(e).start()
            core_d(e).start()

        for e in range(2):
            for t in range(num_tiles):
                in_copy(e, t).start()
            pd[e] = jnp.zeros((8, BLK), F32)

        def first_pass(e, other):
            def body(t, carry):
                in_copy(e, t).wait()
                project(e, t, theta[e, :, tile_ds(t)])
                if other is not None:
                    services(other, t)
                return carry
            lax.fori_loop(0, num_tiles, body, 0)
            send_q(e)
            gram(e)

        def services(o, t):
            @pl.when(t == 0)
            def _():
                stage2_q(o)

            @pl.when(t == 2)
            def _():
                stage2_g(o)

            @pl.when(t == 4)
            def _():
                stage3_q(o)

        def finish(o):
            stage3_g(o)
            stage4(o, (0, 1, 2))
            stage5(o)

        first_pass(0, None)
        first_pass(1, 0)
        finish(0)

        def steady(i, carry):
            e = i % 2
            o = 1 - e

            def body(t, c):
                new = update(e, t)
                project(e, t, new)
                services(o, t)
                return c
            lax.fori_loop(0, num_tiles, body, 0)
            send_q(e)
            gram(e)
            finish(o)
            return carry

        lax.fori_loop(0, 2 * (NUM_STEPS - 1), steady, 0)

        def last0(t, c):
            update(0, t)
            out_copy(0, t).start()
            services(1, t)
            return c
        lax.fori_loop(0, num_tiles, last0, 0)
        finish(1)

        def last1(t, c):
            update(1, t)
            out_copy(1, t).start()
            return c
        lax.fori_loop(0, num_tiles, last1, 0)
        for e in range(2):
            for t in range(num_tiles):
                out_copy(e, t).wait()

    def call(particles, target_mean, precision, low_factor):
        vm = pl.BlockSpec(memory_space=pltpu.VMEM)
        hbm = pl.BlockSpec(memory_space=pl.ANY)
        scratch = [
            pltpu.VMEM((2, num_part, num_local), F32),
            pltpu.VMEM((num_part, num_local), BF16),
            pltpu.VMEM((num_part, num_part), BF16),
            pltpu.VMEM((num_part, BLK), F32),
            pltpu.VMEM((num_part, BLK), F32),
            pltpu.VMEM((2, nblk, BLK, BLK), F32),
            pltpu.VMEM((2, nblk, grow, BLK), F32),
            pltpu.VMEM((2, 8, BLK), F32),
            pltpu.VMEM((2, 2, BLK, BLK), F32),
            pltpu.VMEM((2, 2, grow, BLK), F32),
            pltpu.VMEM((2, 8, BLK), F32),
            pltpu.VMEM((2, 2, BLK, BLK), F32),
            pltpu.VMEM((2, 2, grow, BLK), F32),
            pltpu.VMEM((2, 8, BLK), F32),
            pltpu.VMEM((2, BLK, BLK), F32),
            pltpu.VMEM((2, grow, BLK), F32),
            pltpu.VMEM((2, 8, BLK), F32),
            pltpu.VMEM((8, BLK), F32),
            pltpu.VMEM((grow, BLK), F32),
            pltpu.VMEM((2, num_part, BLK), BF16),
            pltpu.VMEM((2, nblk, grow, BLK), BF16),
            pltpu.VMEM((2, nblk, 8, BLK), F32),
            pltpu.SemaphoreType.DMA((2, num_tiles)),
            pltpu.SemaphoreType.DMA((2, num_tiles)),
            pltpu.SemaphoreType.DMA((2, NUM_SEMS)),
            pltpu.SemaphoreType.DMA((2, NUM_SEMS)),
        ]
        return pl.pallas_call(
            kernel,
            out_shape=jax.ShapeDtypeStruct(particles.shape, F32),
            in_specs=[hbm, vm, vm, vm],
            out_specs=hbm,
            scratch_shapes=scratch,
            compiler_params=pltpu.CompilerParams(
                collective_id=0, has_side_effects=True, vmem_limit_bytes=60 * 1024 * 1024),
            cost_estimate=pl.CostEstimate(flops=33 * 10**9, bytes_accessed=36 * 2**20, transcendentals=0),
        )(particles, target_mean[:, None, :], precision[None, :], low_factor)

    return call


def solution(mesh):
    feat_count = mesh.shape["feat"]
    data_spec = P("ens", None, "feat")

    def local_steps(particles, target_mean, precision, low_factor):
        num_part, num_local = particles.shape[1], particles.shape[2]
        call = build_kernel(num_part, num_local, num_local * feat_count)
        return call(particles, target_mean, precision, low_factor)

    return jax.shard_map(
        local_steps, mesh=mesh,
        in_specs=(data_spec, P("ens", "feat"), P(("ens", "feat")), P(("ens", "feat"), None)),
        out_specs=data_spec, check_vma=False)
```

time: 487 us -> 115 us (0.24); the launches traced: 481 us -> 115 us
  local copies, waits for them, and re-layouts: 198 us -> 13.1 us
  matrix products: 141 us -> 0 us
  Pallas kernels: 0 us -> 102 us
  blocking collectives: 76.4 us -> 0 us
  waiting for transfers between devices: 50 us -> 0 us
  between operations: 13.2 us -> 0.01 us
    psum x3 -> x0, local copies, waits for them, and re-layouts: 181 us -> none  [local_steps(): project, gram_mat = lax.psum((proj_part, gram_part), 'feat')]
    dot_general x12 -> x0, matrix products: 141 us -> none  [the longest x3 46 us: local_steps(): jnp.einsum('enm,emd->end', kernel.astype(jnp.bfloat16), mixed, preferred_...]
    pallas_call x0 -> x1, Pallas kernels: none -> 102 us  [call(): pl.pallas_call(kernel, out_shape=jax.ShapeDtypeStruct(particles.shape, F3...]
    psum x3 -> x0, blocking collectives: 76.4 us -> none  [local_steps(): project, gram_mat = lax.psum((proj_part, gram_part), 'feat')]
    psum x3 -> x0, waiting for transfers between devices: 50 us -> none  [local_steps(): project, gram_mat = lax.psum((proj_part, gram_part), 'feat')]
    gather x6 -> x0, local copies, waits for them, and re-layouts: 16.9 us -> none  [local_steps(): gram_diag = jnp.diagonal(gram_mat, axis1=1, axis2=2)]
    unnamed x12 -> x1, local copies, waits for them, and re-layouts: 0.03 us -> 11.7 us
  transfers between devices with their start and end apart: 3 -> 0, of which waited for: 3 -> 0; matrix products, arithmetic and copies ran while one was open for 8% -> 0% of each run, Pallas kernels for 0% -> 0%
where the time goes in v1:
time: 115 us
  Pallas kernels  102 us (89%)
  local copies, waits for them, and re-layouts  13.1 us (11%)
    pallas_call x1, Pallas kernels, call(): pl.pallas_call(kernel, out_shape=jax.ShapeDtypeStruct(particles.shape, F3...  102 us
    unnamed x1, local copies, waits for them, and re-layouts  11.7 us

profile of v1, /device:TPU:0, one launch (start us, length us, event | category | flops | bytes accessed | tf_op | source)
XLA Modules:
  0.0 115.0 jit_solution(14270462344200243137)
XLA Ops:
  0.0 1.4 %broadcast_in_dim.6.mu_ref = f32[2,1,4096]{2,1,0:T(1,128)} reshape(f32[2,4096]{1,0:T(2,128)} %param.5) | data formatting | bytes 65536 | tf_op jit(solution)/shard_map/broadcast_in_dim | solution.py:352
  1.4 101.9 %shard_map.46 = f32[2,512,4096]{2,1,0:T(8,128)} custom-call(f32[2,512,4096]{2,1,0:T(8,128)} %th_hbm.1, f32[2,1,4096]{2,1,0:T(1,128)} %broadcast_in_dim.6.mu_ref, f32[1,4096]{1,0:T(1,128)} %bitcast.1, bf16[4096,128]{1,0:T(8,128)(2,1)} %u_ref.1), custom_call_target="tpu_custom_call" | custom-call | flops 32999999488 | bytes 37748736 | tf_op jit(solution)/shard_map/pallas_call | solution.py:343
  103.3 11.7 %copy.6 = f32[2,512,4096]{2,1,0:T(8,128)} copy(f32[2,512,4096]{2,1,0:T(8,128)} %shard_map.46) | data formatting | bytes 33554432

commit v2 on v1

--- a/solution.py
+++ b/solution.py
@@ -6,6 +6,10 @@
 from jax.sharding import PartitionSpec as P
 
 NUM_STEPS = 3
+OUT_HBM = True
+POS = 0
+MIX_T = 5
+DRV_T = 1
 BLK = 128
 TILE = 512
 F32 = jnp.float32
@@ -27,7 +31,7 @@
     grow = 2 * BLK + BLK // 2
 
     def kernel(th_hbm, mu_ref, lam_ref, u_ref, out_hbm,
-               theta, tb, kfull, qacc, scol,
+               theta, tb, xb, ybuf, kfull, scol,
                pq, pg, pd, rq, rg, rd, sq, sg, sd, xq, xg, xd, dfull, gsum,
                qall, kall, sall,
                in_sem, out_sem, send_sem, recv_sem):
@@ -37,11 +41,6 @@
         own = 2 * core + chip
         peer_core = {"feat": 2 * chip + (1 - core)}
         peer_chip = {"feat": 2 * (1 - chip) + core}
-
-        barrier = pltpu.get_barrier_semaphore()
-        for peer in (peer_core, peer_chip):
-            pl.semaphore_signal(barrier, inc=1, device_id=peer, device_id_type=pl.DeviceIdType.MESH)
-        pl.semaphore_wait(barrier, 2)
 
         def rcopy(src, dst, e, group, kind, peer):
             idx = group * NUM_KINDS + kind
@@ -150,8 +149,12 @@
                 to_chip(e, kind).wait()
                 forward(e, kind).start()
 
+        def stage5_q(e):
+            to_core(e, 0).wait()
+            forward(e, 0).wait()
+
         def stage5(e):
-            for kind in range(NUM_KINDS):
+            for kind in (1, 2):
                 to_core(e, kind).wait()
                 forward(e, kind).wait()
             half = BLK // 2
@@ -159,58 +162,57 @@
             def put(i, j, rows, block):
                 r0 = i * BLK + rows
                 n = block.shape[0]
-                kfull[r0:r0 + n, j * BLK:(j + 1) * BLK] = block
+                kfull[r0:r0 + n, j * BLK:(j + 1) * BLK] = (block * gain).astype(BF16)
 
             def put_pair(i, j, block):
                 put(i, j, 0, block)
-                put(j, i, 0, block.astype(F32).T.astype(BF16))
+                put(j, i, 0, block.T)
 
             for i in range(nblk):
-                put(i, i, 0, kall[e, i, 0:BLK, :])
+                put(i, i, 0, kall[e, i, 0:BLK, :].astype(F32))
             for i, j, o in ((0, 1, 0), (1, 2, 1), (2, 3, 2), (0, 3, 3)):
-                put_pair(i, j, kall[e, o, BLK:2 * BLK, :])
+                put_pair(i, j, kall[e, o, BLK:2 * BLK, :].astype(F32))
             for i in range(2):
                 lo = kall[e, i, 2 * BLK:2 * BLK + half, :]
                 hi = kall[e, i + 2, 2 * BLK:2 * BLK + half, :]
-                put_pair(i, i + 2, jnp.concatenate([lo, hi], axis=0))
+                put_pair(i, i + 2, jnp.concatenate([lo, hi], axis=0).astype(F32))
             srow = sall[e, 0] + sall[e, 1] + sall[e, 2] + sall[e, 3]
             eye = (lax.broadcasted_iota(jnp.int32, (BLK, BLK), 0) == lax.broadcasted_iota(jnp.int32, (BLK, BLK), 1))
             for i in range(nblk):
                 col = jnp.sum(jnp.where(eye, srow[i:i + 1, :], 0.0), axis=1, keepdims=True)
-                scol[i * BLK:(i + 1) * BLK, :] = jnp.broadcast_to(col, (BLK, BLK)) * two_h
-
-        def project(e, t, value):
+                scol[i * BLK:(i + 1) * BLK, :] = 1.0 + jnp.broadcast_to(col, (BLK, BLK)) * (gain * two_h)
+
+        def round_inputs(e, t, value):
             ds = tile_ds(t)
             tb[:, ds] = value.astype(BF16)
-            xb = (value - mu_ref[e, :, ds]).astype(BF16)
-            part = jnp.dot(xb, u_ref[ds, :], preferred_element_type=F32)
-
-            @pl.when(t == 0)
-            def _():
-                qacc[...] = part
-
-            @pl.when(t > 0)
-            def _():
-                qacc[...] += part
-
-        def update(e, t):
+            xb[:, ds] = (value - mu_ref[pl.ds(e, 1), ds]).astype(BF16)
+
+        def mix(e, t):
             ds = tile_ds(t)
             value = theta[e, :, ds]
             low = lax.dot_general(qall[e], u_ref[ds, :], TRANS_B, preferred_element_type=F32)
-            centered = value - mu_ref[e, :, ds]
-            grad = -(centered * lam_ref[:, ds] + low)
-            mixed = (grad - two_h * value).astype(BF16)
-            drive = jnp.dot(kfull[...], mixed, preferred_element_type=F32)
-            new = value + gain * (drive + scol[:, 0:1] * value)
+            centered = value - mu_ref[pl.ds(e, 1), ds]
+            ybuf[:, ds] = (centered * (lam_ref[:, ds] + two_h) + (low + two_h * mu_ref[pl.ds(e, 1), ds])).astype(BF16)
+
+        def drive(e, t):
+            ds = tile_ds(t)
+            moved = jnp.dot(kfull[...], ybuf[:, ds], preferred_element_type=F32)
+            new = theta[e, :, ds] * scol[:, 0:1] - moved
             theta[e, :, ds] = new
             return new
 
         def send_q(e):
-            for i in range(nblk):
-                pq[e, i] = qacc[i * BLK:(i + 1) * BLK, :]
+            hk = num_local // 2
+
+            @pl.when(feat >= 0)
+            def _():
+                part = [jnp.dot(xb[:, k * hk:(k + 1) * hk], u_ref[k * hk:(k + 1) * hk, :], preferred_element_type=F32) for k in range(2)]
+                part = part[0] + part[1]
+                for i in range(nblk):
+                    pq[e, i] = part[i * BLK:(i + 1) * BLK, :]
             core_q(e).start()
 
-        def gram(e):
+        def gram(e, o):
             half = BLK // 2
             two = 2 * BLK
 
@@ -225,89 +227,101 @@
                 else:
                     pg[e, 3 if (i, j) == (0, 3) else i, BLK:two, :] = block
 
-            right = lax.dot_general(tb[...], tb[two:2 * two, :], TRANS_B, preferred_element_type=F32)
-            for i in range(nblk):
-                for j in (2, 3):
-                    if i <= j:
-                        place(i, j, right[i * BLK:(i + 1) * BLK, (j - 2) * BLK:(j - 1) * BLK])
-            left = lax.dot_general(tb[0:two, :], tb[0:two, :], TRANS_B, preferred_element_type=F32)
-            for i in range(2):
-                for j in range(i, 2):
-                    place(i, j, left[i * BLK:(i + 1) * BLK, j * BLK:(j + 1) * BLK])
+            @pl.when(feat >= 0)
+            def _():
+                right = lax.dot_general(tb[...], tb[two:2 * two, :], TRANS_B, preferred_element_type=F32)
+                left = lax.dot_general(tb[0:two, :], tb[0:two, :], TRANS_B, preferred_element_type=F32)
+                for i in range(nblk):
+                    for j in (2, 3):
+                        if i <= j:
+                            place(i, j, right[i * BLK:(i + 1) * BLK, (j - 2) * BLK:(j - 1) * BLK])
+                for i in range(2):
+                    for j in range(i, 2):
+                        place(i, j, left[i * BLK:(i + 1) * BLK, j * BLK:(j + 1) * BLK])
             core_g(e).start()
             core_d(e).start()
+            stage2_q(e)
+
+        for e in range(2):
+            pd[e] = jnp.zeros((8, BLK), F32)
+
+        def loop(num, body):
+            lax.fori_loop(0, num, lambda t, c: (body(t), c)[1], 0)
+
+        def at(t, when, fn, *args):
+            @pl.when(t == when)
+            def _():
+                fn(*args)
+
+        def first_pass(e):
+            def body(t):
+                in_copy(e, t).wait()
+                round_inputs(e, t, theta[e, :, tile_ds(t)])
+            loop(num_tiles, body)
 
         for e in range(2):
             for t in range(num_tiles):
                 in_copy(e, t).start()
-            pd[e] = jnp.zeros((8, BLK), F32)
-
-        def first_pass(e, other):
-            def body(t, carry):
-                in_copy(e, t).wait()
-                project(e, t, theta[e, :, tile_ds(t)])
-                if other is not None:
-                    services(other, t)
-                return carry
-            lax.fori_loop(0, num_tiles, body, 0)
-            send_q(e)
-            gram(e)
-
-        def services(o, t):
-            @pl.when(t == 0)
-            def _():
-                stage2_q(o)
-
-            @pl.when(t == 2)
-            def _():
-                stage2_g(o)
-
-            @pl.when(t == 4)
-            def _():
-                stage3_q(o)
-
-        def finish(o):
-            stage3_g(o)
-            stage4(o, (0, 1, 2))
-            stage5(o)
-
-        first_pass(0, None)
-        first_pass(1, 0)
-        finish(0)
+        barrier = pltpu.get_barrier_semaphore()
+        for peer in (peer_core, peer_chip):
+            pl.semaphore_signal(barrier, inc=1, device_id=peer, device_id_type=pl.DeviceIdType.MESH)
+        first_pass(0)
+        pl.semaphore_wait(barrier, 2)
+        send_q(0)
+        gram(0, None)
+        first_pass(1)
+        stage2_g(0)
+        send_q(1)
+        stage3_q(0)
+        gram(1, 0)
+        if POS == 0:
+            stage3_g(0)
+        stage4(0, (0,))
+
+        def half_step(e, last, others):
+            o = 1 - e
+            stage5_q(e)
+
+            def mix_body(t):
+                mix(e, t)
+                if others:
+                    at(t, MIX_T, stage2_g, o)
+            loop(num_tiles, mix_body)
+            stage4(e, (1, 2))
+            stage5(e)
+
+            def drive_body(t):
+                new = drive(e, t)
+                if last:
+                    if OUT_HBM:
+                        out_copy(e, t).start()
+                else:
+                    round_inputs(e, t, new)
+                if others:
+                    at(t, DRV_T, stage3_q, o)
+            loop(num_tiles, drive_body)
+            if not last:
+                send_q(e)
+            if others:
+                stage4(o, (0,))
+            if POS == 0 and others:
+                stage3_g(o)
+            if not last:
+                gram(e, o)
+            elif POS == 1 and others:
+                stage3_g(o)
 
         def steady(i, carry):
-            e = i % 2
-            o = 1 - e
-
-            def body(t, c):
-                new = update(e, t)
-                project(e, t, new)
-                services(o, t)
-                return c
-            lax.fori_loop(0, num_tiles, body, 0)
-            send_q(e)
-            gram(e)
-            finish(o)
+            half_step(i % 2, False, True)
             return carry
 
         lax.fori_loop(0, 2 * (NUM_STEPS - 1), steady, 0)
-
-        def last0(t, c):
-            update(0, t)
-            out_copy(0, t).start()
-            services(1, t)
-            return c
-        lax.fori_loop(0, num_tiles, last0, 0)
-        finish(1)
-
-        def last1(t, c):
-            update(1, t)
-            out_copy(1, t).start()
-            return c
-        lax.fori_loop(0, num_tiles, last1, 0)
-        for e in range(2):
-            for t in range(num_tiles):
-                out_copy(e, t).wait()
+        half_step(0, True, True)
+        half_step(1, True, False)
+        if OUT_HBM:
+            for e in range(2):
+                for t in range(num_tiles):
+                    out_copy(e, t).wait()
 
     def call(particles, target_mean, precision, low_factor):
         vm = pl.BlockSpec(memory_space=pltpu.VMEM)
@@ -315,8 +329,9 @@
         scratch = [
             pltpu.VMEM((2, num_part, num_local), F32),
             pltpu.VMEM((num_part, num_local), BF16),
+            pltpu.VMEM((num_part, num_local), BF16),
+            pltpu.VMEM((num_part, num_local), BF16),
             pltpu.VMEM((num_part, num_part), BF16),
-            pltpu.VMEM((num_part, BLK), F32),
             pltpu.VMEM((num_part, BLK), F32),
             pltpu.VMEM((2, nblk, BLK, BLK), F32),
             pltpu.VMEM((2, nblk, grow, BLK), F32),
@@ -349,7 +364,7 @@
             compiler_params=pltpu.CompilerParams(
                 collective_id=0, has_side_effects=True, vmem_limit_bytes=60 * 1024 * 1024),
             cost_estimate=pl.CostEstimate(flops=33 * 10**9, bytes_accessed=36 * 2**20, transcendentals=0),
-        )(particles, target_mean[:, None, :], precision[None, :], low_factor)
+        )(particles, target_mean, precision[None, :], low_factor)
 
     return call
 

time: 115 us -> 93.4 us (0.81)
  Pallas kernels: 102 us -> 81.5 us
  local copies, waits for them, and re-layouts: 13.1 us -> 11.7 us
    pallas_call x1, Pallas kernels: 102 us -> 81.5 us  [call(): pl.pallas_call(kernel, out_shape=jax.ShapeDtypeStruct(particles.shape, F3...]
    broadcast_in_dim x1 -> x0, local copies, waits for them, and re-layouts: 1.39 us -> none  [call(): target_mean[:, None, :]]
where the time goes in v2:
time: 93.4 us; the launch traced here: 93.2 us
  Pallas kernels  81.5 us (87%)
  local copies, waits for them, and re-layouts  11.7 us (13%)
    pallas_call x1, Pallas kernels, call(): pl.pallas_call(kernel, out_shape=jax.ShapeDtypeStruct(particles.shape, F3...  81.5 us
    unnamed x1, local copies, waits for them, and re-layouts  11.7 us

profile of v2, /device:TPU:0, one launch (start us, length us, event | category | flops | bytes accessed | tf_op | source)
XLA Modules:
  0.0 93.2 jit_solution(15341059421082508184)
XLA Ops:
  0.0 81.5 %shard_map.46 = f32[2,512,4096]{2,1,0:T(8,128)} custom-call(f32[2,512,4096]{2,1,0:T(8,128)} %th_hbm.1, f32[2,4096]{1,0:T(2,128)} %mu_ref.1, f32[1,4096]{1,0:T(1,128)} %bitcast.1, bf16[4096,128]{1,0:T(8,128)(2,1)} %u_ref.1), custom_call_target="tpu_custom_call" | custom-call | flops 32999999488 | bytes 37748736 | tf_op jit(solution)/shard_map/pallas_call | solution.py:358
  81.5 11.7 %copy.6 = f32[2,512,4096]{2,1,0:T(8,128)} copy(f32[2,512,4096]{2,1,0:T(8,128)} %shard_map.46) | data formatting | bytes 33554432

commit v3 on v2

--- a/solution.py
+++ b/solution.py
@@ -6,8 +6,6 @@
 from jax.sharding import PartitionSpec as P
 
 NUM_STEPS = 3
-OUT_HBM = True
-POS = 0
 MIX_T = 5
 DRV_T = 1
 BLK = 128
@@ -30,11 +28,11 @@
     gain = step_size / num_part
     grow = 2 * BLK + BLK // 2
 
-    def kernel(th_hbm, mu_ref, lam_ref, u_ref, out_hbm,
-               theta, tb, xb, ybuf, kfull, scol,
+    def kernel(th_hbm, mu_ref, lam_ref, u_ref, theta, ybuf, kfull, scol,
+               tb, xb,
                pq, pg, pd, rq, rg, rd, sq, sg, sd, xq, xg, xd, dfull, gsum,
                qall, kall, sall,
-               in_sem, out_sem, send_sem, recv_sem):
+               in_sem, send_sem, recv_sem):
         feat = lax.axis_index("feat")
         chip = feat // 2
         core = feat % 2
@@ -53,9 +51,6 @@
 
         def in_copy(e, t):
             return pltpu.make_async_copy(th_hbm.at[e, :, tile_ds(t)], theta.at[e, :, tile_ds(t)], in_sem.at[e, t])
-
-        def out_copy(e, t):
-            return pltpu.make_async_copy(theta.at[e, :, tile_ds(t)], out_hbm.at[e, :, tile_ds(t)], out_sem.at[e, t])
 
         def core_q(e):
             return rcopy(pq.at[e, pl.ds(2 * (1 - core), 2)], rq.at[e], e, SEM_CORE, 0, peer_core)
@@ -212,7 +207,7 @@
                     pq[e, i] = part[i * BLK:(i + 1) * BLK, :]
             core_q(e).start()
 
-        def gram(e, o):
+        def gram(e):
             half = BLK // 2
             two = 2 * BLK
 
@@ -268,71 +263,77 @@
         first_pass(0)
         pl.semaphore_wait(barrier, 2)
         send_q(0)
-        gram(0, None)
+        gram(0)
         first_pass(1)
         stage2_g(0)
         send_q(1)
         stage3_q(0)
-        gram(1, 0)
-        if POS == 0:
-            stage3_g(0)
+        gram(1)
+        stage3_g(0)
         stage4(0, (0,))
 
-        def half_step(e, last, others):
-            o = 1 - e
+        def finish_mix(e, o):
             stage5_q(e)
 
             def mix_body(t):
                 mix(e, t)
-                if others:
+                if o is not None:
                     at(t, MIX_T, stage2_g, o)
             loop(num_tiles, mix_body)
             stage4(e, (1, 2))
             stage5(e)
 
+        def half_step(e, last):
+            o = 1 - e
+            finish_mix(e, o)
+
             def drive_body(t):
                 new = drive(e, t)
-                if last:
-                    if OUT_HBM:
-                        out_copy(e, t).start()
-                else:
+                if not last:
                     round_inputs(e, t, new)
-                if others:
-                    at(t, DRV_T, stage3_q, o)
+                at(t, DRV_T, stage3_q, o)
             loop(num_tiles, drive_body)
             if not last:
                 send_q(e)
-            if others:
-                stage4(o, (0,))
-            if POS == 0 and others:
-                stage3_g(o)
+            stage4(o, (0,))
+            stage3_g(o)
             if not last:
-                gram(e, o)
-            elif POS == 1 and others:
-                stage3_g(o)
+                gram(e)
 
         def steady(i, carry):
-            half_step(i % 2, False, True)
+            half_step(i % 2, False)
             return carry
 
         lax.fori_loop(0, 2 * (NUM_STEPS - 1), steady, 0)
-        half_step(0, True, True)
-        half_step(1, True, False)
-        if OUT_HBM:
-            for e in range(2):
-                for t in range(num_tiles):
-                    out_copy(e, t).wait()
+        half_step(0, True)
+        finish_mix(1, None)
+
+    def last_kernel(theta, ybuf, kfull, scol, out_hbm, new, out_sem):
+        first = pltpu.make_async_copy(theta.at[0], out_hbm.at[0], out_sem.at[num_tiles])
+        first.start()
+
+        def out_copy(t):
+            ds = pl.ds(pl.multiple_of(t * TILE, TILE), TILE)
+            return pltpu.make_async_copy(new.at[:, ds], out_hbm.at[1, :, ds], out_sem.at[t])
+
+        def body(t, carry):
+            ds = pl.ds(pl.multiple_of(t * TILE, TILE), TILE)
+            moved = jnp.dot(kfull[...], ybuf[:, ds], preferred_element_type=F32)
+            new[:, ds] = theta[1, :, ds] * scol[:, 0:1] - moved
+            out_copy(t).start()
+            return carry
+
+        lax.fori_loop(0, num_tiles, body, 0)
+        first.wait()
+        for t in range(num_tiles):
+            out_copy(t).wait()
 
     def call(particles, target_mean, precision, low_factor):
         vm = pl.BlockSpec(memory_space=pltpu.VMEM)
         hbm = pl.BlockSpec(memory_space=pl.ANY)
         scratch = [
-            pltpu.VMEM((2, num_part, num_local), F32),
             pltpu.VMEM((num_part, num_local), BF16),
             pltpu.VMEM((num_part, num_local), BF16),
-            pltpu.VMEM((num_part, num_local), BF16),
-            pltpu.VMEM((num_part, num_part), BF16),
-            pltpu.VMEM((num_part, BLK), F32),
             pltpu.VMEM((2, nblk, BLK, BLK), F32),
             pltpu.VMEM((2, nblk, grow, BLK), F32),
             pltpu.VMEM((2, 8, BLK), F32),
@@ -351,20 +352,29 @@
             pltpu.VMEM((2, nblk, grow, BLK), BF16),
             pltpu.VMEM((2, nblk, 8, BLK), F32),
             pltpu.SemaphoreType.DMA((2, num_tiles)),
-            pltpu.SemaphoreType.DMA((2, num_tiles)),
             pltpu.SemaphoreType.DMA((2, NUM_SEMS)),
             pltpu.SemaphoreType.DMA((2, NUM_SEMS)),
         ]
-        return pl.pallas_call(
+        state = pl.pallas_call(
             kernel,
-            out_shape=jax.ShapeDtypeStruct(particles.shape, F32),
+            out_shape=(pltpu.VMEM(particles.shape, F32), pltpu.VMEM((num_part, num_local), BF16),
+                       pltpu.VMEM((num_part, num_part), BF16), pltpu.VMEM((num_part, BLK), F32)),
             in_specs=[hbm, vm, vm, vm],
-            out_specs=hbm,
+            out_specs=(vm, vm, vm, vm),
             scratch_shapes=scratch,
             compiler_params=pltpu.CompilerParams(
-                collective_id=0, has_side_effects=True, vmem_limit_bytes=60 * 1024 * 1024),
-            cost_estimate=pl.CostEstimate(flops=33 * 10**9, bytes_accessed=36 * 2**20, transcendentals=0),
+                collective_id=0, has_side_effects=True, vmem_limit_bytes=36 * 1024 * 1024),
+            cost_estimate=pl.CostEstimate(flops=30 * 10**9, bytes_accessed=18 * 2**20, transcendentals=0),
         )(particles, target_mean, precision[None, :], low_factor)
+        return pl.pallas_call(
+            last_kernel,
+            out_shape=jax.ShapeDtypeStruct(particles.shape, F32),
+            in_specs=[vm, vm, vm, vm],
+            out_specs=hbm,
+            scratch_shapes=[pltpu.VMEM((num_part, num_local), F32), pltpu.SemaphoreType.DMA((num_tiles + 1,))],
+            compiler_params=pltpu.CompilerParams(vmem_limit_bytes=10 * 1024 * 1024),
+            cost_estimate=pl.CostEstimate(flops=2 * 10**9, bytes_accessed=16 * 2**20, transcendentals=0),
+        )(*state)
 
     return call
 

time: 93.4 us -> 82.9 us (0.89)
  local copies, waits for them, and re-layouts: 11.7 us -> 0 us
  Pallas kernels: 81.5 us -> 82.8 us
    unnamed x1 -> x0, local copies, waits for them, and re-layouts: 11.7 us -> none
    pallas_call x1 -> x2, Pallas kernels: 81.5 us -> 82.8 us  [the longest x1 76.8 us: call(): pl.pallas_call(kernel, out_shape=(pltpu.VMEM(particles.shape, F32), pltpu...]
where the time goes in v3:
time: 82.9 us; the launch traced here: 82.8 us
  Pallas kernels  82.8 us (100%)
    pallas_call x1, Pallas kernels, call(): pl.pallas_call(kernel, out_shape=(pltpu.VMEM(particles.shape, F32), pltpu...  76.8 us
    pallas_call x1, Pallas kernels, call(): pl.pallas_call(last_kernel, out_shape=jax.ShapeDtypeStruct(particles.shap...  6.02 us

profile of v3, /device:TPU:0, one launch (start us, length us, event | category | flops | bytes accessed | tf_op | source)
XLA Modules:
  0.0 82.8 jit_solution(3165720900958197035)
XLA Ops:
  0.0 76.8 %shard_map.46 = (f32[2,512,4096]{2,1,0:T(8,128)S(1)}, bf16[512,4096]{1,0:T(8,128)(2,1)S(1)}, bf16[512,512]{1,0:T(8,128)(2,1)S(1)}, f32[512,128]{1,0:T(8,128)S(1)}) custom-call(f32[2,512,4096]{2,1,0:T(8,128)} %th_hbm.1, f32[2,4096]{1,0:T(2,128)} %mu_ref.1, f32[1,4096]{1,0:T(1,128)} %bitcast.1, bf16[4096,128]{1,0:T(8,128)(2,1)} %u_ref.1), custom_call_target="tpu_custom_call" | custom-call | flops 30000001024 | bytes 18874368 | tf_op jit(solution)/shard_map/pallas_call | solution.py:358
  76.8 6.0 %shard_map.47 = f32[2,512,4096]{2,1,0:T(8,128)} custom-call(f32[2,512,4096]{2,1,0:T(8,128)S(1)} %get-tuple-element.9.theta, bf16[512,4096]{1,0:T(8,128)(2,1)S(1)} %get-tuple-element.10.ybuf, bf16[512,512]{1,0:T(8,128)(2,1)S(1)} %get-tuple-element.11.kfull, f32[512,128]{1,0:T(8,128)S(1)} %get-tuple-element.12.scol), custom_call_target="tpu_custom_call" | custom-call | flops 2000000000 | bytes 16777216 | tf_op jit(solution)/shard_map/pallas_call | solution.py:369

commit v4 on v3

v4 whole, which is shorter than its diff:
```python
import jax
import jax.numpy as jnp
from jax import lax
from jax.experimental import pallas as pl
from jax.experimental.pallas import tpu as pltpu
from jax.sharding import PartitionSpec as P

NUM_STEPS = 3
BLK = 128
TILE = 512
MTILE = 1024
DTILE = 2048
T2D = 1
T4O = 1
T2O = 2
S3 = 0
F32 = jnp.float32
BF16 = jnp.bfloat16
TRANS_B = (((1,), (1,)), ((), ()))

SEM_CORE, SEM_CHIP, SEM_GATHER, SEM_OWN, SEM_FWD = range(5)
KIND_Q, KIND_DIAG, KIND_OFF, KIND_VEC = range(4)
NUM_KINDS = 4
NUM_SEMS = 5 * NUM_KINDS


def build_kernel(num_part, num_local, total_feat):
    nblk = num_part // BLK
    num_tiles = num_local // TILE
    bandwidth = 2.0 * total_feat
    step_size = 0.25 * total_feat
    two_h = 2.0 / bandwidth
    gain = step_size / num_part
    piece = BLK // nblk
    diag_blocks = ((0, 0), (0, 1), (1, 1), (2, 2), (2, 3), (3, 3))
    off_blocks = ((0, 2), (0, 3), (1, 2), (1, 3))
    blocks = diag_blocks + off_blocks
    grow = piece * len(blocks)
    split = piece * len(diag_blocks)
    spans = {KIND_DIAG: pl.ds(0, split), KIND_OFF: pl.ds(split, grow - split)}

    def kernel(th_hbm, mu_ref, lam_ref, u_ref, theta, ybuf, kfull, scol,
               tb, xb,
               pq, pg, pd, rq, rg, rd, sq, sg, sd, xq, xg, xd, dfull,
               qall, kall, sall,
               in_sem, send_sem, recv_sem):
        feat = lax.axis_index("feat")
        chip = feat // 2
        core = feat % 2
        own = 2 * core + chip
        peer_core = {"feat": 2 * chip + (1 - core)}
        peer_chip = {"feat": 2 * (1 - chip) + core}

        def rcopy(src, dst, e, group, kind, peer):
            idx = group * NUM_KINDS + kind
            return pltpu.make_async_remote_copy(
                src_ref=src, dst_ref=dst, send_sem=send_sem.at[e, idx], recv_sem=recv_sem.at[e, idx],
                device_id=peer, device_id_type=pl.DeviceIdType.MESH)

        def tile_ds(t, size=TILE):
            return pl.ds(pl.multiple_of(t * size, size), size)

        def in_copy(e, t):
            return pltpu.make_async_copy(th_hbm.at[e, :, tile_ds(t)], theta.at[e, :, tile_ds(t)], in_sem.at[e, t])

        def core_reduce(e, kind):
            if kind == KIND_Q:
                src, dst = pq.at[e, pl.ds(2 * (1 - core), 2)], rq.at[e]
            elif kind == KIND_VEC:
                src, dst = pd.at[e], rd.at[e]
            else:
                src, dst = pg.at[e, pl.ds(2 * (1 - core), 2), spans[kind]], rg.at[e, :, spans[kind]]
            return rcopy(src, dst, e, SEM_CORE, kind, peer_core)

        def chip_reduce(e, kind):
            if kind == KIND_Q:
                src, dst = sq.at[e, 1 - chip], xq.at[e]
            elif kind == KIND_VEC:
                src, dst = sd.at[e], xd.at[e]
            else:
                src, dst = sg.at[e, 1 - chip, spans[kind]], xg.at[e, spans[kind]]
            return rcopy(src, dst, e, SEM_CHIP, kind, peer_chip)

        def gather(e, slot, group, kind, peer):
            if kind == KIND_Q:
                ref = qall.at[e, pl.ds(pl.multiple_of(slot * BLK, BLK), BLK)]
            elif kind == KIND_VEC:
                ref = sall.at[e, slot]
            else:
                ref = kall.at[e, slot, spans[kind]]
            return rcopy(ref, ref, e, group, kind, peer)

        def to_chip(e, kind):
            return gather(e, own, SEM_GATHER, kind, peer_chip)

        def to_core(e, kind):
            return gather(e, own, SEM_OWN, kind, peer_core)

        def forward(e, kind):
            return gather(e, 2 * core + (1 - chip), SEM_FWD, kind, peer_core)

        def stage2_q(e):
            core_reduce(e, KIND_Q).wait()
            for c in range(2):
                sq[e, c] = pq[e, 2 * core + c] + rq[e, c]
            chip_reduce(e, KIND_Q).start()

        def stage2_g(e, kind):
            if kind == KIND_DIAG:
                core_reduce(e, KIND_VEC).wait()
                sd[e] = pd[e] + rd[e]
                chip_reduce(e, KIND_VEC).start()
            core_reduce(e, kind).wait()
            for c in range(2):
                sg[e, c, spans[kind], :] = pg[e, 2 * core + c, spans[kind], :] + rg[e, c, spans[kind], :]
            chip_reduce(e, kind).start()

        def stage3_q(e):
            chip_reduce(e, KIND_Q).wait()
            full = sq[e, chip] + xq[e]
            qall[e, pl.ds(pl.multiple_of(own * BLK, BLK), BLK), :] = full.astype(BF16)
            to_chip(e, KIND_Q).start()
            to_core(e, KIND_Q).start()

        def stage3_g(e, kind):
            if kind == KIND_DIAG:
                chip_reduce(e, KIND_VEC).wait()
                dfull[...] = sd[e] + xd[e]
                first, last = 0, len(diag_blocks)
            else:
                first, last = len(diag_blocks), len(blocks)
            chip_reduce(e, kind).wait()
            row_id = lax.broadcasted_iota(jnp.int32, (piece, BLK), 0) + own * piece
            col_id = lax.broadcasted_iota(jnp.int32, (piece, BLK), 1)
            mine = row_id == col_id
            diag_cols = {}
            col_sums = [None] * nblk
            for index in range(first, last):
                i, j = blocks[index]
                rows = slice(index * piece, (index + 1) * piece)
                if i not in diag_cols:
                    diag_cols[i] = jnp.sum(jnp.where(mine, dfull[i:i + 1, :], 0.0), axis=1, keepdims=True)
                gram_rows = sg[e, chip, rows, :] + xg[e, rows, :]
                dist = jnp.maximum(diag_cols[i] + dfull[j:j + 1, :] - 2.0 * gram_rows, 0.0)
                kern = jnp.exp(-dist / bandwidth)
                kall[e, own, rows, :] = kern.astype(BF16)
                adds = [(j, kern)]
                if i != j:
                    adds.append((i, jnp.where(mine, jnp.sum(kern, axis=1, keepdims=True), 0.0)))
                for b, term in adds:
                    col_sums[b] = term if col_sums[b] is None else col_sums[b] + term
            for b in range(nblk):
                total = jnp.sum(col_sums[b], axis=0, keepdims=True)
                if kind == KIND_OFF:
                    total = total + sall[e, own, b:b + 1, :]
                sall[e, own, b:b + 1, :] = total
            for k in (kind,) if kind == KIND_DIAG else (kind, KIND_VEC):
                to_chip(e, k).start()
                to_core(e, k).start()

        def stage4(e, kinds):
            for kind in kinds:
                to_chip(e, kind).wait()
                forward(e, kind).start()

        def arrived(e, kind):
            to_core(e, kind).wait()
            forward(e, kind).wait()

        def stage5_q(e):
            arrived(e, KIND_Q)

        def stage5(e, kind):
            arrived(e, kind)
            for index, (i, j) in enumerate(blocks):
                if (index < len(diag_blocks)) != (kind == KIND_DIAG):
                    continue
                rows = slice(index * piece, (index + 1) * piece)
                block = jnp.concatenate([kall[e, o, rows, :].astype(F32) for o in range(nblk)], axis=0) * gain
                kfull[i * BLK:(i + 1) * BLK, j * BLK:(j + 1) * BLK] = block.astype(BF16)
                if i != j:
                    kfull[j * BLK:(j + 1) * BLK, i * BLK:(i + 1) * BLK] = block.T.astype(BF16)
            if kind == KIND_OFF:
                arrived(e, KIND_VEC)
                srow = sall[e, 0] + sall[e, 1] + sall[e, 2] + sall[e, 3]
                eye = (lax.broadcasted_iota(jnp.int32, (BLK, BLK), 0) == lax.broadcasted_iota(jnp.int32, (BLK, BLK), 1))
                for i in range(nblk):
                    col = jnp.sum(jnp.where(eye, srow[i:i + 1, :], 0.0), axis=1, keepdims=True)
                    scol[i * BLK:(i + 1) * BLK, :] = 1.0 + jnp.broadcast_to(col, (BLK, BLK)) * (gain * two_h)

        def round_inputs(e, ds, value):
            tb[:, ds] = value.astype(BF16)
            xb[:, ds] = (value - mu_ref[pl.ds(e, 1), ds]).astype(BF16)

        def mix(e, t):
            ds = tile_ds(t, MTILE)
            value = theta[e, :, ds]
            low = lax.dot_general(qall[e], u_ref[ds, :], TRANS_B, preferred_element_type=F32)
            centered = value - mu_ref[pl.ds(e, 1), ds]
            ybuf[:, ds] = (centered * (lam_ref[:, ds] + two_h) + (low + two_h * mu_ref[pl.ds(e, 1), ds])).astype(BF16)

        def drive(e, t):
            ds = tile_ds(t, DTILE)
            moved = jnp.dot(kfull[...], ybuf[:, ds], preferred_element_type=F32)
            new = theta[e, :, ds] * scol[:, 0:1] - moved
            theta[e, :, ds] = new
            return new

        def send_q(e):
            hk = num_local // 2

            @pl.when(feat >= 0)
            def _():
                part = [jnp.dot(xb[:, k * hk:(k + 1) * hk], u_ref[k * hk:(k + 1) * hk, :], preferred_element_type=F32) for k in range(2)]
                part = part[0] + part[1]
                for i in range(nblk):
                    pq[e, i] = part[i * BLK:(i + 1) * BLK, :]
            core_reduce(e, KIND_Q).start()

        def gram(e, kind):
            two = 2 * BLK
            hk = num_local // 2
            eye = (lax.broadcasted_iota(jnp.int32, (BLK, BLK), 0) == lax.broadcasted_iota(jnp.int32, (BLK, BLK), 1))

            def place(i, j, block):
                index = blocks.index((i, j))
                for o in range(nblk):
                    pg[e, o, index * piece:(index + 1) * piece, :] = block[o * piece:(o + 1) * piece]
                if i == j:
                    pd[e, i:i + 1, :] = jnp.sum(jnp.where(eye, block, 0.0), axis=0, keepdims=True)

            @pl.when(feat >= 0)
            def _():
                if kind == KIND_DIAG:
                    for half in range(2):
                        rows = tb[half * two:(half + 1) * two, :]
                        prod = lax.dot_general(rows, rows, TRANS_B, preferred_element_type=F32)
                        for i in range(2):
                            for j in range(i, 2):
                                place(2 * half + i, 2 * half + j, prod[i * BLK:(i + 1) * BLK, j * BLK:(j + 1) * BLK])
                else:
                    prod = [lax.dot_general(tb[0:two, k * hk:(k + 1) * hk], tb[two:2 * two, k * hk:(k + 1) * hk], TRANS_B,
                                            preferred_element_type=F32) for k in range(2)]
                    prod = prod[0] + prod[1]
                    for i in range(2):
                        for j in range(2):
                            place(i, 2 + j, prod[i * BLK:(i + 1) * BLK, j * BLK:(j + 1) * BLK])
            core_reduce(e, kind).start()
            if kind == KIND_DIAG:
                core_reduce(e, KIND_VEC).start()

        for e in range(2):
            pd[e] = jnp.zeros((8, BLK), F32)

        def loop(num, body):
            lax.fori_loop(0, num, lambda t, c: (body(t), c)[1], 0)

        def at(t, when, fn, *args):
            @pl.when(t == when)
            def _():
                fn(*args)

        def first_pass(e):
            def body(t):
                in_copy(e, t).wait()
                round_inputs(e, tile_ds(t), theta[e, :, tile_ds(t)])
            loop(num_tiles, body)

        for e in range(2):
            for t in range(num_tiles):
                in_copy(e, t).start()
        barrier = pltpu.get_barrier_semaphore()
        for peer in (peer_core, peer_chip):
            pl.semaphore_signal(barrier, inc=1, device_id=peer, device_id_type=pl.DeviceIdType.MESH)
        def send_gram(e):
            gram(e, KIND_DIAG)
            stage2_q(e)
            gram(e, KIND_OFF)

        first_pass(0)
        pl.semaphore_wait(barrier, 2)
        send_q(0)
        send_gram(0)
        first_pass(1)
        stage2_g(0, KIND_DIAG)
        stage2_g(0, KIND_OFF)
        send_q(1)
        stage3_q(0)
        gram(1, KIND_DIAG)
        stage2_q(1)
        gram(1, KIND_OFF)
        stage3_g(0, KIND_DIAG)
        stage3_g(0, KIND_OFF)
        stage4(0, (KIND_Q,))

        def finish_mix(e, o):
            stage5_q(e)
            if o is not None:
                stage4(e, (KIND_DIAG,))

            def mix_body(t):
                mix(e, t)
                if o is not None:
                    at(t, T2D, stage2_g, o, KIND_DIAG)
                    at(t, T4O, stage4, e, (KIND_OFF, KIND_VEC))
                    at(t, T2O, stage2_g, o, KIND_OFF)
            loop(num_local // MTILE, mix_body)
            if o is None:
                stage4(e, (KIND_DIAG, KIND_OFF, KIND_VEC))
            stage5(e, KIND_DIAG)
            stage5(e, KIND_OFF)

        def half_step(e, last):
            o = 1 - e
            finish_mix(e, o)

            def drive_body(t):
                new = drive(e, t)
                if not last:
                    round_inputs(e, tile_ds(t, DTILE), new)
                at(t, 0, stage3_q, o)
            loop(num_local // DTILE, drive_body)
            if S3 == 0:
                stage3_g(o, KIND_DIAG)
            if not last:
                send_q(e)
            stage4(o, (KIND_Q,))
            if S3 == 1:
                stage3_g(o, KIND_DIAG)
            stage3_g(o, KIND_OFF)
            if not last:
                send_gram(e)

        def steady(i, carry):
            half_step(i % 2, False)
            return carry

        lax.fori_loop(0, 2 * (NUM_STEPS - 1), steady, 0)
        half_step(0, True)
        finish_mix(1, None)

    def last_kernel(theta, ybuf, kfull, scol, out_hbm, new, out_sem):
        first = pltpu.make_async_copy(theta.at[0], out_hbm.at[0], out_sem.at[num_tiles])
        first.start()

        def out_copy(t):
            ds = pl.ds(pl.multiple_of(t * TILE, TILE), TILE)
            return pltpu.make_async_copy(new.at[:, ds], out_hbm.at[1, :, ds], out_sem.at[t])

        def body(t, carry):
            ds = pl.ds(pl.multiple_of(t * TILE, TILE), TILE)
            moved = jnp.dot(kfull[...], ybuf[:, ds], preferred_element_type=F32)
            new[:, ds] = theta[1, :, ds] * scol[:, 0:1] - moved
            out_copy(t).start()
            return carry

        lax.fori_loop(0, num_tiles, body, 0)
        first.wait()
        for t in range(num_tiles):
            out_copy(t).wait()

    def call(particles, target_mean, precision, low_factor):
        vm = pl.BlockSpec(memory_space=pltpu.VMEM)
        hbm = pl.BlockSpec(memory_space=pl.ANY)
        scratch = [
            pltpu.VMEM((num_part, num_local), BF16),
            pltpu.VMEM((num_part, num_local), BF16),
            pltpu.VMEM((2, nblk, BLK, BLK), F32),
            pltpu.VMEM((2, nblk, grow, BLK), F32),
            pltpu.VMEM((2, 8, BLK), F32),
            pltpu.VMEM((2, 2, BLK, BLK), F32),
            pltpu.VMEM((2, 2, grow, BLK), F32),
            pltpu.VMEM((2, 8, BLK), F32),
            pltpu.VMEM((2, 2, BLK, BLK), F32),
            pltpu.VMEM((2, 2, grow, BLK), F32),
            pltpu.VMEM((2, 8, BLK), F32),
            pltpu.VMEM((2, BLK, BLK), F32),
            pltpu.VMEM((2, grow, BLK), F32),
            pltpu.VMEM((2, 8, BLK), F32),
            pltpu.VMEM((8, BLK), F32),
            pltpu.VMEM((2, num_part, BLK), BF16),
            pltpu.VMEM((2, nblk, grow, BLK), BF16),
            pltpu.VMEM((2, nblk, 8, BLK), F32),
            pltpu.SemaphoreType.DMA((2, num_tiles)),
            pltpu.SemaphoreType.DMA((2, NUM_SEMS)),
            pltpu.SemaphoreType.DMA((2, NUM_SEMS)),
        ]
        state = pl.pallas_call(
            kernel,
            out_shape=(pltpu.VMEM(particles.shape, F32), pltpu.VMEM((num_part, num_local), BF16),
                       pltpu.VMEM((num_part, num_part), BF16), pltpu.VMEM((num_part, BLK), F32)),
            in_specs=[hbm, vm, vm, vm],
            out_specs=(vm, vm, vm, vm),
            scratch_shapes=scratch,
            compiler_params=pltpu.CompilerParams(
                collective_id=0, has_side_effects=True, vmem_limit_bytes=36 * 1024 * 1024),
            cost_estimate=pl.CostEstimate(flops=30 * 10**9, bytes_accessed=18 * 2**20, transcendentals=0),
        )(particles, target_mean, precision[None, :], low_factor)
        return pl.pallas_call(
            last_kernel,
            out_shape=jax.ShapeDtypeStruct(particles.shape, F32),
            in_specs=[vm, vm, vm, vm],
            out_specs=hbm,
            scratch_shapes=[pltpu.VMEM((num_part, num_local), F32), pltpu.SemaphoreType.DMA((num_tiles + 1,))],
            compiler_params=pltpu.CompilerParams(vmem_limit_bytes=10 * 1024 * 1024),
            cost_estimate=pl.CostEstimate(flops=2 * 10**9, bytes_accessed=16 * 2**20, transcendentals=0),
        )(*state)

    return call


def solution(mesh):
    feat_count = mesh.shape["feat"]
    data_spec = P("ens", None, "feat")

    def local_steps(particles, target_mean, precision, low_factor):
        num_part, num_local = particles.shape[1], particles.shape[2]
        call = build_kernel(num_part, num_local, num_local * feat_count)
        return call(particles, target_mean, precision, low_factor)

    return jax.shard_map(
        local_steps, mesh=mesh,
        in_specs=(data_spec, P("ens", "feat"), P(("ens", "feat")), P(("ens", "feat"), None)),
        out_specs=data_spec, check_vma=False)
```

time: 82.9 us -> 75.6 us (0.912)
  Pallas kernels: 82.8 us -> 75.3 us
    pallas_call x1, Pallas kernels: 76.8 us -> 69.3 us  [call(): pl.pallas_call(kernel, out_shape=(pltpu.VMEM(particles.shape, F32), pltpu...]
where the time goes in v4:
time: 75.6 us; the launch traced here: 75.5 us
  Pallas kernels  75.3 us (100%)
    pallas_call x1, Pallas kernels, call(): pl.pallas_call(kernel, out_shape=(pltpu.VMEM(particles.shape, F32), pltpu...  69.3 us
    pallas_call x1, Pallas kernels, call(): pl.pallas_call(last_kernel, out_shape=jax.ShapeDtypeStruct(particles.shap...  6.02 us

profile of v4, /device:TPU:0, one launch (start us, length us, event | category | flops | bytes accessed | tf_op | source)
XLA Modules:
  0.0 75.5 jit_solution(13812595785882310044)
XLA Ops:
  0.0 69.3 %shard_map.46 = (f32[2,512,4096]{2,1,0:T(8,128)S(1)}, bf16[512,4096]{1,0:T(8,128)(2,1)S(1)}, bf16[512,512]{1,0:T(8,128)(2,1)S(1)}, f32[512,128]{1,0:T(8,128)S(1)}) custom-call(f32[2,512,4096]{2,1,0:T(8,128)} %th_hbm.1, f32[2,4096]{1,0:T(2,128)} %mu_ref.1, f32[1,4096]{1,0:T(1,128)} %bitcast.1, bf16[4096,128]{1,0:T(8,128)(2,1)} %u_ref.1), custom_call_target="tpu_custom_call" | custom-call | flops 30000001024 | bytes 18874368 | tf_op jit(solution)/shard_map/pallas_call | solution.py:388
  69.3 6.0 %shard_map.47 = f32[2,512,4096]{2,1,0:T(8,128)} custom-call(f32[2,512,4096]{2,1,0:T(8,128)S(1)} %get-tuple-element.9.theta, bf16[512,4096]{1,0:T(8,128)(2,1)S(1)} %get-tuple-element.10.ybuf, bf16[512,512]{1,0:T(8,128)(2,1)S(1)} %get-tuple-element.11.kfull, f32[512,128]{1,0:T(8,128)S(1)} %get-tuple-element.12.scol), custom_call_target="tpu_custom_call" | custom-call | flops 2000000000 | bytes 16777216 | tf_op jit(solution)/shard_map/pallas_call | solution.py:399

commit v5 on v4

--- a/solution.py
+++ b/solution.py
@@ -7,13 +7,17 @@
 
 NUM_STEPS = 3
 BLK = 128
-TILE = 512
-MTILE = 1024
+TILE = 1024
+OUT_TILE = 512
+MTILE = 2048
 DTILE = 2048
-T2D = 1
-T4O = 1
-T2O = 2
-S3 = 0
+T2D = 0
+T4O = 0
+T2O = 1
+LTILE = 1024
+L3D = 2
+P2Q = 0
+P2O = 0
 F32 = jnp.float32
 BF16 = jnp.bfloat16
 TRANS_B = (((1,), (1,)), ((), ()))
@@ -32,18 +36,18 @@
     two_h = 2.0 / bandwidth
     gain = step_size / num_part
     piece = BLK // nblk
-    diag_blocks = ((0, 0), (0, 1), (1, 1), (2, 2), (2, 3), (3, 3))
-    off_blocks = ((0, 2), (0, 3), (1, 2), (1, 3))
+    diag_blocks = ((0, 1, True), (2, 3, True), (0, 1, False), (2, 3, False))
+    off_blocks = ((0, 2, False), (0, 3, False), (1, 2, False), (1, 3, False))
     blocks = diag_blocks + off_blocks
     grow = piece * len(blocks)
     split = piece * len(diag_blocks)
     spans = {KIND_DIAG: pl.ds(0, split), KIND_OFF: pl.ds(split, grow - split)}
 
-    def kernel(th_hbm, mu_ref, lam_ref, u_ref, theta, ybuf, kfull, scol,
-               tb, xb,
+    def kernel(th_hbm, mu_hbm, lam_hbm, u_hbm, theta, ybuf, kfull, scol,
+               tb,
                pq, pg, pd, rq, rg, rd, sq, sg, sd, xq, xg, xd, dfull,
                qall, kall, sall,
-               in_sem, send_sem, recv_sem):
+               mu_ref, lam_ref, u_ref, in_sem, par_sem, send_sem, recv_sem):
         feat = lax.axis_index("feat")
         chip = feat // 2
         core = feat % 2
@@ -121,6 +125,13 @@
             qall[e, pl.ds(pl.multiple_of(own * BLK, BLK), BLK), :] = full.astype(BF16)
             to_chip(e, KIND_Q).start()
             to_core(e, KIND_Q).start()
+
+        def kernel_of(norm, value):
+            return jnp.exp(-jnp.maximum(norm - 2.0 * value, 0.0) / bandwidth)
+
+        def kernel_diag(b):
+            norm = dfull[b:b + 1, :]
+            return kernel_of(norm + norm, norm)
 
         def stage3_g(e, kind):
             if kind == KIND_DIAG:
@@ -133,22 +144,43 @@
             row_id = lax.broadcasted_iota(jnp.int32, (piece, BLK), 0) + own * piece
             col_id = lax.broadcasted_iota(jnp.int32, (piece, BLK), 1)
             mine = row_id == col_id
+            upper, lower = row_id < col_id, row_id > col_id
             diag_cols = {}
             col_sums = [None] * nblk
+
+            def diag_row(b):
+                return dfull[b:b + 1, :]
+
+            def diag_col(b):
+                if b not in diag_cols:
+                    diag_cols[b] = jnp.sum(jnp.where(mine, diag_row(b), 0.0), axis=1, keepdims=True)
+                return diag_cols[b]
+
+            def add(b, term):
+                col_sums[b] = term if col_sums[b] is None else col_sums[b] + term
+
+            def add_rows(b, term):
+                add(b, jnp.where(mine, jnp.sum(term, axis=1, keepdims=True), 0.0))
+
             for index in range(first, last):
-                i, j = blocks[index]
+                i, j, packed = blocks[index]
                 rows = slice(index * piece, (index + 1) * piece)
-                if i not in diag_cols:
-                    diag_cols[i] = jnp.sum(jnp.where(mine, dfull[i:i + 1, :], 0.0), axis=1, keepdims=True)
                 gram_rows = sg[e, chip, rows, :] + xg[e, rows, :]
-                dist = jnp.maximum(diag_cols[i] + dfull[j:j + 1, :] - 2.0 * gram_rows, 0.0)
-                kern = jnp.exp(-dist / bandwidth)
-                kall[e, own, rows, :] = kern.astype(BF16)
-                adds = [(j, kern)]
-                if i != j:
-                    adds.append((i, jnp.where(mine, jnp.sum(kern, axis=1, keepdims=True), 0.0)))
-                for b, term in adds:
-                    col_sums[b] = term if col_sums[b] is None else col_sums[b] + term
+                if packed:
+                    norm = jnp.where(lower, diag_col(j) + diag_row(j), diag_col(i) + diag_row(i))
+                else:
+                    norm = diag_col(i) + diag_row(j)
+                kern = kernel_of(norm, gram_rows)
+                kall[e, own, rows, :] = (kern * gain).astype(BF16)
+                if packed:
+                    kern_up, kern_low = jnp.where(upper, kern, 0.0), jnp.where(lower, kern, 0.0)
+                    add(i, jnp.where(lower, 0.0, kern))
+                    add_rows(i, kern_up)
+                    add(j, kern_low + jnp.where(mine, kernel_diag(j), 0.0))
+                    add_rows(j, kern_low)
+                else:
+                    add(j, kern)
+                    add_rows(i, kern)
             for b in range(nblk):
                 total = jnp.sum(col_sums[b], axis=0, keepdims=True)
                 if kind == KIND_OFF:
@@ -172,14 +204,25 @@
 
         def stage5(e, kind):
             arrived(e, kind)
-            for index, (i, j) in enumerate(blocks):
+            row_id = lax.broadcasted_iota(jnp.int32, (BLK, BLK), 0)
+            col_id = lax.broadcasted_iota(jnp.int32, (BLK, BLK), 1)
+
+            def put(i, j, value):
+                kfull[i * BLK:(i + 1) * BLK, j * BLK:(j + 1) * BLK] = value.astype(BF16)
+
+            for index, (i, j, packed) in enumerate(blocks):
                 if (index < len(diag_blocks)) != (kind == KIND_DIAG):
                     continue
                 rows = slice(index * piece, (index + 1) * piece)
-                block = jnp.concatenate([kall[e, o, rows, :].astype(F32) for o in range(nblk)], axis=0) * gain
-                kfull[i * BLK:(i + 1) * BLK, j * BLK:(j + 1) * BLK] = block.astype(BF16)
-                if i != j:
-                    kfull[j * BLK:(j + 1) * BLK, i * BLK:(i + 1) * BLK] = block.T.astype(BF16)
+                block = jnp.concatenate([kall[e, o, rows, :].astype(F32) for o in range(nblk)], axis=0)
+                flipped = block.T
+                if packed:
+                    put(i, i, jnp.where(row_id <= col_id, block, flipped))
+                    rest = jnp.where(row_id < col_id, flipped, (kernel_diag(j) * gain).astype(BF16).astype(F32))
+                    put(j, j, jnp.where(row_id > col_id, block, rest))
+                else:
+                    put(i, j, block)
+                    put(j, i, flipped)
             if kind == KIND_OFF:
                 arrived(e, KIND_VEC)
                 srow = sall[e, 0] + sall[e, 1] + sall[e, 2] + sall[e, 3]
@@ -190,7 +233,6 @@
 
         def round_inputs(e, ds, value):
             tb[:, ds] = value.astype(BF16)
-            xb[:, ds] = (value - mu_ref[pl.ds(e, 1), ds]).astype(BF16)
 
         def mix(e, t):
             ds = tile_ds(t, MTILE)
@@ -199,55 +241,87 @@
             centered = value - mu_ref[pl.ds(e, 1), ds]
             ybuf[:, ds] = (centered * (lam_ref[:, ds] + two_h) + (low + two_h * mu_ref[pl.ds(e, 1), ds])).astype(BF16)
 
-        def drive(e, t):
-            ds = tile_ds(t, DTILE)
+        def drive(e, ds):
             moved = jnp.dot(kfull[...], ybuf[:, ds], preferred_element_type=F32)
             new = theta[e, :, ds] * scol[:, 0:1] - moved
             theta[e, :, ds] = new
             return new
 
-        def send_q(e):
-            hk = num_local // 2
-
+        def q_dot(e, ds_a, ds_b):
+            parts = [jnp.dot((theta[e, :, d] - mu_ref[pl.ds(e, 1), d]).astype(BF16), u_ref[d, :], preferred_element_type=F32) for d in (ds_a, ds_b)]
+            return parts[0] + parts[1]
+
+        def gram_dots(kind, ds_all, ds_a, ds_b):
+            two = 2 * BLK
+            out = {}
+            if kind == KIND_DIAG:
+                for half in range(2):
+                    rows = tb[half * two:(half + 1) * two, ds_all]
+                    prod = lax.dot_general(rows, rows, TRANS_B, preferred_element_type=F32)
+                    for i in range(2):
+                        for j in range(i, 2):
+                            out[2 * half + i, 2 * half + j] = prod[i * BLK:(i + 1) * BLK, j * BLK:(j + 1) * BLK]
+            else:
+                prod = [lax.dot_general(tb[0:two, d], tb[two:2 * two, d], TRANS_B, preferred_element_type=F32)
+                        for d in (ds_a, ds_b)]
+                prod = prod[0] + prod[1]
+                for i in range(2):
+                    for j in range(2):
+                        out[i, 2 + j] = prod[i * BLK:(i + 1) * BLK, j * BLK:(j + 1) * BLK]
+            return out
+
+        def put_q(e, value):
+            for i in range(nblk):
+                pq[e, i] = value[i * BLK:(i + 1) * BLK, :]
+
+        def put_gram(e, kind, out, add):
+            row_id = lax.broadcasted_iota(jnp.int32, (BLK, BLK), 0)
+            col_id = lax.broadcasted_iota(jnp.int32, (BLK, BLK), 1)
+            for index, (i, j, packed) in enumerate(blocks):
+                if (index < len(diag_blocks)) != (kind == KIND_DIAG):
+                    continue
+                block = jnp.where(row_id <= col_id, out[i, i], out[j, j]) if packed else out[i, j]
+                for o in range(nblk):
+                    rows = slice(index * piece, (index + 1) * piece)
+                    term = block[o * piece:(o + 1) * piece]
+                    pg[e, o, rows, :] = pg[e, o, rows, :] + term if add else term
+            if kind == KIND_DIAG:
+                for i in range(nblk):
+                    term = jnp.sum(jnp.where(row_id == col_id, out[i, i], 0.0), axis=0, keepdims=True)
+                    pd[e, i:i + 1, :] = pd[e, i:i + 1, :] + term if add else term
+
+        def first_chunk(e, c):
+            half = TILE // 2
+            in_copy(e, c).wait()
+            round_inputs(e, tile_ds(c), theta[e, :, tile_ds(c)])
+            start = pl.multiple_of(c * TILE, TILE)
+            ds_a, ds_b = pl.ds(start, half), pl.ds(start + half, half)
+            for kind in (KIND_DIAG, KIND_OFF):
+                put_gram(e, kind, gram_dots(kind, tile_ds(c), ds_a, ds_b), True)
+
+        def send(e, kinds):
+            for kind in kinds:
+                core_reduce(e, kind).start()
+
+        half_a, half_b, whole = pl.ds(0, num_local // 2), pl.ds(num_local // 2, num_local // 2), pl.ds(0, num_local)
+
+        def sums_1(e):
             @pl.when(feat >= 0)
             def _():
-                part = [jnp.dot(xb[:, k * hk:(k + 1) * hk], u_ref[k * hk:(k + 1) * hk, :], preferred_element_type=F32) for k in range(2)]
-                part = part[0] + part[1]
-                for i in range(nblk):
-                    pq[e, i] = part[i * BLK:(i + 1) * BLK, :]
-            core_reduce(e, KIND_Q).start()
-
-        def gram(e, kind):
-            two = 2 * BLK
-            hk = num_local // 2
-            eye = (lax.broadcasted_iota(jnp.int32, (BLK, BLK), 0) == lax.broadcasted_iota(jnp.int32, (BLK, BLK), 1))
-
-            def place(i, j, block):
-                index = blocks.index((i, j))
-                for o in range(nblk):
-                    pg[e, o, index * piece:(index + 1) * piece, :] = block[o * piece:(o + 1) * piece]
-                if i == j:
-                    pd[e, i:i + 1, :] = jnp.sum(jnp.where(eye, block, 0.0), axis=0, keepdims=True)
-
+                put_q(e, q_dot(e, half_a, half_b))
+            send(e, (KIND_Q,))
+
+        def sums_2(e):
             @pl.when(feat >= 0)
             def _():
-                if kind == KIND_DIAG:
-                    for half in range(2):
-                        rows = tb[half * two:(half + 1) * two, :]
-                        prod = lax.dot_general(rows, rows, TRANS_B, preferred_element_type=F32)
-                        for i in range(2):
-                            for j in range(i, 2):
-                                place(2 * half + i, 2 * half + j, prod[i * BLK:(i + 1) * BLK, j * BLK:(j + 1) * BLK])
-                else:
-                    prod = [lax.dot_general(tb[0:two, k * hk:(k + 1) * hk], tb[two:2 * two, k * hk:(k + 1) * hk], TRANS_B,
-                                            preferred_element_type=F32) for k in range(2)]
-                    prod = prod[0] + prod[1]
-                    for i in range(2):
-                        for j in range(2):
-                            place(i, 2 + j, prod[i * BLK:(i + 1) * BLK, j * BLK:(j + 1) * BLK])
-            core_reduce(e, kind).start()
-            if kind == KIND_DIAG:
-                core_reduce(e, KIND_VEC).start()
+                put_gram(e, KIND_DIAG, gram_dots(KIND_DIAG, whole, half_a, half_b), False)
+            send(e, (KIND_VEC, KIND_DIAG))
+            stage2_q(e)
+
+            @pl.when(feat >= 0)
+            def _():
+                put_gram(e, KIND_OFF, gram_dots(KIND_OFF, whole, half_a, half_b), False)
+            send(e, (KIND_OFF,))
 
         for e in range(2):
             pd[e] = jnp.zeros((8, BLK), F32)
@@ -260,15 +334,16 @@
             def _():
                 fn(*args)
 
-        def first_pass(e):
-            def body(t):
-                in_copy(e, t).wait()
-                round_inputs(e, tile_ds(t), theta[e, :, tile_ds(t)])
-            loop(num_tiles, body)
-
-        for e in range(2):
-            for t in range(num_tiles):
-                in_copy(e, t).start()
+        def par_copy(index):
+            src, dst = ((mu_hbm, mu_ref), (lam_hbm, lam_ref), (u_hbm, u_ref))[index]
+            return pltpu.make_async_copy(src, dst, par_sem.at[index])
+
+        for c in range(num_tiles):
+            in_copy(0, c).start()
+        for index in range(3):
+            par_copy(index).start()
+        for c in range(num_tiles):
+            in_copy(1, c).start()
         barrier = pltpu.get_barrier_semaphore()
         for peer in (peer_core, peer_chip):
             pl.semaphore_signal(barrier, inc=1, device_id=peer, device_id_type=pl.DeviceIdType.MESH)
@@ -277,93 +352,104 @@
             stage2_q(e)
             gram(e, KIND_OFF)
 
-        first_pass(0)
+        for e in range(2):
+            pg[e] = jnp.zeros((nblk, grow, BLK), F32)
+        loop(num_tiles, lambda c: first_chunk(0, c))
+        par_copy(0).wait()
+        par_copy(2).wait()
         pl.semaphore_wait(barrier, 2)
-        send_q(0)
-        send_gram(0)
-        first_pass(1)
+        send(0, (KIND_VEC, KIND_DIAG, KIND_OFF))
+        sums_1(0)
         stage2_g(0, KIND_DIAG)
-        stage2_g(0, KIND_OFF)
-        send_q(1)
+
+        def second_pass(c):
+            first_chunk(1, c)
+            at(c, P2Q, stage2_q, 0)
+            at(c, P2O, stage2_g, 0, KIND_OFF)
+        loop(num_tiles, second_pass)
+        send(1, (KIND_VEC, KIND_DIAG, KIND_OFF))
+        stage3_g(0, KIND_DIAG)
         stage3_q(0)
-        gram(1, KIND_DIAG)
-        stage2_q(1)
-        gram(1, KIND_OFF)
-        stage3_g(0, KIND_DIAG)
+        sums_1(1)
         stage3_g(0, KIND_OFF)
         stage4(0, (KIND_Q,))
+        stage2_q(1)
+        par_copy(1).wait()
 
         def finish_mix(e, o):
             stage5_q(e)
-            if o is not None:
-                stage4(e, (KIND_DIAG,))
+            stage4(e, (KIND_DIAG,))
 
             def mix_body(t):
                 mix(e, t)
+                at(t, T4O, stage4, e, (KIND_OFF, KIND_VEC))
                 if o is not None:
                     at(t, T2D, stage2_g, o, KIND_DIAG)
-                    at(t, T4O, stage4, e, (KIND_OFF, KIND_VEC))
                     at(t, T2O, stage2_g, o, KIND_OFF)
             loop(num_local // MTILE, mix_body)
-            if o is None:
-                stage4(e, (KIND_DIAG, KIND_OFF, KIND_VEC))
             stage5(e, KIND_DIAG)
             stage5(e, KIND_OFF)
 
-        def half_step(e, last):
+        def half_step(e):
             o = 1 - e
             finish_mix(e, o)
 
             def drive_body(t):
-                new = drive(e, t)
-                if not last:
-                    round_inputs(e, tile_ds(t, DTILE), new)
+                round_inputs(e, tile_ds(t, DTILE), drive(e, tile_ds(t, DTILE)))
                 at(t, 0, stage3_q, o)
             loop(num_local // DTILE, drive_body)
-            if S3 == 0:
-                stage3_g(o, KIND_DIAG)
-            if not last:
-                send_q(e)
+            stage3_g(o, KIND_DIAG)
+            sums_1(e)
             stage4(o, (KIND_Q,))
-            if S3 == 1:
-                stage3_g(o, KIND_DIAG)
             stage3_g(o, KIND_OFF)
-            if not last:
-                send_gram(e)
+            sums_2(e)
+
+        def last_half_step():
+            finish_mix(0, 1)
+
+            stage3_q(1)
+
+            def drive_body(t):
+                drive(0, tile_ds(t, LTILE))
+                at(t, L3D, stage3_g, 1, KIND_DIAG)
+            loop(num_local // LTILE, drive_body)
+            stage3_g(1, KIND_OFF)
+            stage4(1, (KIND_Q,))
+            finish_mix(1, None)
 
         def steady(i, carry):
-            half_step(i % 2, False)
+            half_step(i % 2)
             return carry
 
         lax.fori_loop(0, 2 * (NUM_STEPS - 1), steady, 0)
-        half_step(0, True)
-        finish_mix(1, None)
+        last_half_step()
+
+    out_tiles = num_local // OUT_TILE
 
     def last_kernel(theta, ybuf, kfull, scol, out_hbm, new, out_sem):
-        first = pltpu.make_async_copy(theta.at[0], out_hbm.at[0], out_sem.at[num_tiles])
+        first = pltpu.make_async_copy(theta.at[0], out_hbm.at[0], out_sem.at[out_tiles])
         first.start()
 
         def out_copy(t):
-            ds = pl.ds(pl.multiple_of(t * TILE, TILE), TILE)
+            ds = pl.ds(pl.multiple_of(t * OUT_TILE, OUT_TILE), OUT_TILE)
             return pltpu.make_async_copy(new.at[:, ds], out_hbm.at[1, :, ds], out_sem.at[t])
 
         def body(t, carry):
-            ds = pl.ds(pl.multiple_of(t * TILE, TILE), TILE)
+            ds = pl.ds(pl.multiple_of(t * OUT_TILE, OUT_TILE), OUT_TILE)
             moved = jnp.dot(kfull[...], ybuf[:, ds], preferred_element_type=F32)
             new[:, ds] = theta[1, :, ds] * scol[:, 0:1] - moved
             out_copy(t).start()
             return carry
 
-        lax.fori_loop(0, num_tiles, body, 0)
+        lax.fori_loop(0, out_tiles, body, 0)
         first.wait()
-        for t in range(num_tiles):
+        for t in range(out_tiles):
             out_copy(t).wait()
 
     def call(particles, target_mean, precision, low_factor):
         vm = pl.BlockSpec(memory_space=pltpu.VMEM)
-        hbm = pl.BlockSpec(memory_space=pl.ANY)
+        hbm = pl.BlockSpec(memory_space=pltpu.HBM)
         scratch = [
-            pltpu.VMEM((num_part, num_local), BF16),
             pltpu.VMEM((num_part, num_local), BF16),
             pltpu.VMEM((2, nblk, BLK, BLK), F32),
             pltpu.VMEM((2, nblk, grow, BLK), F32),
@@ -381,7 +467,11 @@
             pltpu.VMEM((2, num_part, BLK), BF16),
             pltpu.VMEM((2, nblk, grow, BLK), BF16),
             pltpu.VMEM((2, nblk, 8, BLK), F32),
+            pltpu.VMEM((2, num_local), F32),
+            pltpu.VMEM((1, num_local), F32),
+            pltpu.VMEM((num_local, BLK), BF16),
             pltpu.SemaphoreType.DMA((2, num_tiles)),
+            pltpu.SemaphoreType.DMA((3,)),
             pltpu.SemaphoreType.DMA((2, NUM_SEMS)),
             pltpu.SemaphoreType.DMA((2, NUM_SEMS)),
         ]
@@ -389,7 +479,7 @@
             kernel,
             out_shape=(pltpu.VMEM(particles.shape, F32), pltpu.VMEM((num_part, num_local), BF16),
                        pltpu.VMEM((num_part, num_part), BF16), pltpu.VMEM((num_part, BLK), F32)),
-            in_specs=[hbm, vm, vm, vm],
+            in_specs=[hbm, hbm, hbm, hbm],
             out_specs=(vm, vm, vm, vm),
             scratch_shapes=scratch,
             compiler_params=pltpu.CompilerParams(
@@ -401,7 +491,7 @@
             out_shape=jax.ShapeDtypeStruct(particles.shape, F32),
             in_specs=[vm, vm, vm, vm],
             out_specs=hbm,
-            scratch_shapes=[pltpu.VMEM((num_part, num_local), F32), pltpu.SemaphoreType.DMA((num_tiles + 1,))],
+            scratch_shapes=[pltpu.VMEM((num_part, num_local), F32), pltpu.SemaphoreType.DMA((out_tiles + 1,))],
             compiler_params=pltpu.CompilerParams(vmem_limit_bytes=10 * 1024 * 1024),
             cost_estimate=pl.CostEstimate(flops=2 * 10**9, bytes_accessed=16 * 2**20, transcendentals=0),
         )(*state)

time: 75.6 us -> 69.7 us (0.922)
  Pallas kernels: 75.3 us -> 69.6 us
    pallas_call x1, Pallas kernels: 69.3 us -> 63.6 us  [call(): pl.pallas_call(kernel, out_shape=(pltpu.VMEM(particles.shape, F32), pltpu...]
where the time goes in v5:
time: 69.7 us
  Pallas kernels  69.6 us (100%)
    pallas_call x1, Pallas kernels, call(): pl.pallas_call(kernel, out_shape=(pltpu.VMEM(particles.shape, F32), pltpu...  63.6 us
    pallas_call x1, Pallas kernels, call(): pl.pallas_call(last_kernel, out_shape=jax.ShapeDtypeStruct(particles.shap...  6.02 us

profile of v5, /device:TPU:0, one launch (start us, length us, event | category | flops | bytes accessed | tf_op | source)
XLA Modules:
  0.0 69.7 jit_solution(12288104294347377861)
XLA Ops:
  0.0 63.6 %shard_map.46 = (f32[2,512,4096]{2,1,0:T(8,128)S(1)}, bf16[512,4096]{1,0:T(8,128)(2,1)S(1)}, bf16[512,512]{1,0:T(8,128)(2,1)S(1)}, f32[512,128]{1,0:T(8,128)S(1)}) custom-call(f32[2,512,4096]{2,1,0:T(8,128)} %th_hbm.1, f32[2,4096]{1,0:T(2,128)} %mu_hbm.1, f32[1,4096]{1,0:T(1,128)} %bitcast.1, bf16[4096,128]{1,0:T(8,128)(2,1)} %u_hbm.1), custom_call_target="tpu_custom_call" | custom-call | flops 30000001024 | bytes 18874368 | tf_op jit(solution)/shard_map/pallas_call | solution.py:478
  63.6 6.0 %shard_map.47 = f32[2,512,4096]{2,1,0:T(8,128)} custom-call(f32[2,512,4096]{2,1,0:T(8,128)S(1)} %get-tuple-element.9.theta, bf16[512,4096]{1,0:T(8,128)(2,1)S(1)} %get-tuple-element.10.ybuf, bf16[512,512]{1,0:T(8,128)(2,1)S(1)} %get-tuple-element.11.kfull, f32[512,128]{1,0:T(8,128)S(1)} %get-tuple-element.12.scol), custom_call_target="tpu_custom_call" | custom-call | flops 2000000000 | bytes 16777216 | tf_op jit(solution)/shard_map/pallas_call | solution.py:489

commit v6 on v5

--- a/solution.py
+++ b/solution.py
@@ -25,6 +25,7 @@
 SEM_CORE, SEM_CHIP, SEM_GATHER, SEM_OWN, SEM_FWD = range(5)
 KIND_Q, KIND_DIAG, KIND_OFF, KIND_VEC = range(4)
 NUM_KINDS = 4
+DIRECT = (KIND_DIAG, KIND_OFF, KIND_VEC)
 NUM_SEMS = 5 * NUM_KINDS
 
 
@@ -54,6 +55,7 @@
         own = 2 * core + chip
         peer_core = {"feat": 2 * chip + (1 - core)}
         peer_chip = {"feat": 2 * (1 - chip) + core}
+        peer_cross = {"feat": 2 * (1 - chip) + (1 - core)}
 
         def rcopy(src, dst, e, group, kind, peer):
             idx = group * NUM_KINDS + kind
@@ -99,6 +101,15 @@
 
         def to_core(e, kind):
             return gather(e, own, SEM_OWN, kind, peer_core)
+
+        def to_cross(e, kind):
+            return gather(e, own, SEM_FWD, kind, peer_cross)
+
+        def start_gather(e, kind):
+            to_chip(e, kind).start()
+            if kind in DIRECT:
+                to_cross(e, kind).start()
+            to_core(e, kind).start()
 
         def forward(e, kind):
             return gather(e, 2 * core + (1 - chip), SEM_FWD, kind, peer_core)
@@ -123,8 +134,7 @@
             chip_reduce(e, KIND_Q).wait()
             full = sq[e, chip] + xq[e]
             qall[e, pl.ds(pl.multiple_of(own * BLK, BLK), BLK), :] = full.astype(BF16)
-            to_chip(e, KIND_Q).start()
-            to_core(e, KIND_Q).start()
+            start_gather(e, KIND_Q)
 
         def kernel_of(norm, value):
             return jnp.exp(-jnp.maximum(norm - 2.0 * value, 0.0) / bandwidth)
@@ -187,17 +197,21 @@
                     total = total + sall[e, own, b:b + 1, :]
                 sall[e, own, b:b + 1, :] = total
             for k in (kind,) if kind == KIND_DIAG else (kind, KIND_VEC):
-                to_chip(e, k).start()
-                to_core(e, k).start()
+                start_gather(e, k)
 
         def stage4(e, kinds):
             for kind in kinds:
-                to_chip(e, kind).wait()
-                forward(e, kind).start()
+                if kind not in DIRECT:
+                    to_chip(e, kind).wait()
+                    forward(e, kind).start()
 
         def arrived(e, kind):
             to_core(e, kind).wait()
-            forward(e, kind).wait()
+            if kind in DIRECT:
+                to_chip(e, kind).wait()
+                to_cross(e, kind).wait()
+            else:
+                forward(e, kind).wait()
 
         def stage5_q(e):
             arrived(e, KIND_Q)
@@ -342,10 +356,8 @@
             in_copy(0, c).start()
         for index in range(3):
             par_copy(index).start()
-        for c in range(num_tiles):
-            in_copy(1, c).start()
         barrier = pltpu.get_barrier_semaphore()
-        for peer in (peer_core, peer_chip):
+        for peer in (peer_core, peer_chip, peer_cross):
             pl.semaphore_signal(barrier, inc=1, device_id=peer, device_id_type=pl.DeviceIdType.MESH)
         def send_gram(e):
             gram(e, KIND_DIAG)
@@ -354,10 +366,13 @@
 
         for e in range(2):
             pg[e] = jnp.zeros((nblk, grow, BLK), F32)
-        loop(num_tiles, lambda c: first_chunk(0, c))
+        def first_pass(c):
+            first_chunk(0, c)
+            in_copy(1, c).start()
+        loop(num_tiles, first_pass)
         par_copy(0).wait()
         par_copy(2).wait()
-        pl.semaphore_wait(barrier, 2)
+        pl.semaphore_wait(barrier, 3)
         send(0, (KIND_VEC, KIND_DIAG, KIND_OFF))
         sums_1(0)
         stage2_g(0, KIND_DIAG)
@@ -368,8 +383,8 @@
             at(c, P2O, stage2_g, 0, KIND_OFF)
         loop(num_tiles, second_pass)
         send(1, (KIND_VEC, KIND_DIAG, KIND_OFF))
+        stage3_q(0)
         stage3_g(0, KIND_DIAG)
-        stage3_q(0)
         sums_1(1)
         stage3_g(0, KIND_OFF)
         stage4(0, (KIND_Q,))
@@ -407,10 +422,9 @@
         def last_half_step():
             finish_mix(0, 1)
 
-            stage3_q(1)
-
             def drive_body(t):
                 drive(0, tile_ds(t, LTILE))
+                at(t, 0, stage3_q, 1)
                 at(t, L3D, stage3_g, 1, KIND_DIAG)
             loop(num_local // LTILE, drive_body)
             stage3_g(1, KIND_OFF)
@@ -427,8 +441,12 @@
     out_tiles = num_local // OUT_TILE
 
     def last_kernel(theta, ybuf, kfull, scol, out_hbm, new, out_sem):
-        first = pltpu.make_async_copy(theta.at[0], out_hbm.at[0], out_sem.at[out_tiles])
-        first.start()
+        def first(t):
+            ds = pl.ds(t * (num_part // out_tiles), num_part // out_tiles)
+            return pltpu.make_async_copy(theta.at[0, ds], out_hbm.at[0, ds], out_sem.at[out_tiles + t])
+
+        for t in range(out_tiles):
+            first(t).start()
 
         def out_copy(t):
             ds = pl.ds(pl.multiple_of(t * OUT_TILE, OUT_TILE), OUT_TILE)
@@ -442,8 +460,8 @@
             return carry
 
         lax.fori_loop(0, out_tiles, body, 0)
-        first.wait()
         for t in range(out_tiles):
+            first(t).wait()
             out_copy(t).wait()
 
     def call(particles, target_mean, precision, low_factor):
@@ -491,7 +509,7 @@
             out_shape=jax.ShapeDtypeStruct(particles.shape, F32),
             in_specs=[vm, vm, vm, vm],
             out_specs=hbm,
-            scratch_shapes=[pltpu.VMEM((num_part, num_local), F32), pltpu.SemaphoreType.DMA((out_tiles + 1,))],
+            scratch_shapes=[pltpu.VMEM((num_part, num_local), F32), pltpu.SemaphoreType.DMA((2 * out_tiles,))],
             compiler_params=pltpu.CompilerParams(vmem_limit_bytes=10 * 1024 * 1024),
             cost_estimate=pl.CostEstimate(flops=2 * 10**9, bytes_accessed=16 * 2**20, transcendentals=0),
         )(*state)

time: 69.7 us -> 67.7 us (0.971)
  Pallas kernels: 69.6 us -> 67.6 us
    pallas_call x1, Pallas kernels: 63.6 us -> 61.7 us  [call(): pl.pallas_call(kernel, out_shape=(pltpu.VMEM(particles.shape, F32), pltpu...]
where the time goes in v6:
time: 67.7 us; the launch traced here: 67.6 us
  Pallas kernels  67.6 us (100%)
    pallas_call x1, Pallas kernels, call(): pl.pallas_call(kernel, out_shape=(pltpu.VMEM(particles.shape, F32), pltpu...  61.7 us
    pallas_call x1, Pallas kernels, call(): pl.pallas_call(last_kernel, out_shape=jax.ShapeDtypeStruct(particles.shap...  5.96 us

profile of v6, /device:TPU:0, one launch (start us, length us, event | category | flops | bytes accessed | tf_op | source)
XLA Modules:
  0.0 67.6 jit_solution(991427920606696773)
XLA Ops:
  0.0 61.7 %shard_map.46 = (f32[2,512,4096]{2,1,0:T(8,128)S(1)}, bf16[512,4096]{1,0:T(8,128)(2,1)S(1)}, bf16[512,512]{1,0:T(8,128)(2,1)S(1)}, f32[512,128]{1,0:T(8,128)S(1)}) custom-call(f32[2,512,4096]{2,1,0:T(8,128)} %th_hbm.1, f32[2,4096]{1,0:T(2,128)} %mu_hbm.1, f32[1,4096]{1,0:T(1,128)} %bitcast.1, bf16[4096,128]{1,0:T(8,128)(2,1)} %u_hbm.1), custom_call_target="tpu_custom_call" | custom-call | flops 30000001024 | bytes 18874368 | tf_op jit(solution)/shard_map/pallas_call | solution.py:496
  61.7 6.0 %shard_map.47 = f32[2,512,4096]{2,1,0:T(8,128)} custom-call(f32[2,512,4096]{2,1,0:T(8,128)S(1)} %get-tuple-element.9.theta, bf16[512,4096]{1,0:T(8,128)(2,1)S(1)} %get-tuple-element.10.ybuf, bf16[512,512]{1,0:T(8,128)(2,1)S(1)} %get-tuple-element.11.kfull, f32[512,128]{1,0:T(8,128)S(1)} %get-tuple-element.12.scol), custom_call_target="tpu_custom_call" | custom-call | flops 2000000000 | bytes 16777216 | tf_op jit(solution)/shard_map/pallas_call | solution.py:507

commit v7 on v6

--- a/solution.py
+++ b/solution.py
@@ -11,6 +11,7 @@
 OUT_TILE = 512
 MTILE = 2048
 DTILE = 2048
+MIX_TILES = (2048, 2048)
 T2D = 0
 T4O = 0
 T2O = 1
@@ -228,15 +229,16 @@
                 if (index < len(diag_blocks)) != (kind == KIND_DIAG):
                     continue
                 rows = slice(index * piece, (index + 1) * piece)
-                block = jnp.concatenate([kall[e, o, rows, :].astype(F32) for o in range(nblk)], axis=0)
-                flipped = block.T
                 if packed:
+                    block = jnp.concatenate([kall[e, o, rows, :].astype(F32) for o in range(nblk)], axis=0)
+                    flipped = block.T
                     put(i, i, jnp.where(row_id <= col_id, block, flipped))
                     rest = jnp.where(row_id < col_id, flipped, (kernel_diag(j) * gain).astype(BF16).astype(F32))
                     put(j, j, jnp.where(row_id > col_id, block, rest))
                 else:
+                    block = jnp.concatenate([kall[e, o, rows, :] for o in range(nblk)], axis=0)
                     put(i, j, block)
-                    put(j, i, flipped)
+                    put(j, i, block.T)
             if kind == KIND_OFF:
                 arrived(e, KIND_VEC)
                 srow = sall[e, 0] + sall[e, 1] + sall[e, 2] + sall[e, 3]
@@ -248,8 +250,7 @@
         def round_inputs(e, ds, value):
             tb[:, ds] = value.astype(BF16)
 
-        def mix(e, t):
-            ds = tile_ds(t, MTILE)
+        def mix(e, ds):
             value = theta[e, :, ds]
             low = lax.dot_general(qall[e], u_ref[ds, :], TRANS_B, preferred_element_type=F32)
             centered = value - mu_ref[pl.ds(e, 1), ds]
@@ -395,13 +396,18 @@
             stage5_q(e)
             stage4(e, (KIND_DIAG,))
 
-            def mix_body(t):
-                mix(e, t)
-                at(t, T4O, stage4, e, (KIND_OFF, KIND_VEC))
-                if o is not None:
-                    at(t, T2D, stage2_g, o, KIND_DIAG)
-                    at(t, T2O, stage2_g, o, KIND_OFF)
-            loop(num_local // MTILE, mix_body)
+            start = 0
+            for t, size in enumerate(MIX_TILES):
+                @pl.when(feat >= 0)
+                def _():
+                    mix(e, pl.ds(start, size))
+                start += size
+                if t == T4O:
+                    stage4(e, (KIND_OFF, KIND_VEC))
+                if o is not None and t == T2D:
+                    stage2_g(o, KIND_DIAG)
+                if o is not None and t == T2O:
+                    stage2_g(o, KIND_OFF)
             stage5(e, KIND_DIAG)
             stage5(e, KIND_OFF)
 
@@ -415,8 +421,8 @@
             loop(num_local // DTILE, drive_body)
             stage3_g(o, KIND_DIAG)
             sums_1(e)
+            stage3_g(o, KIND_OFF)
             stage4(o, (KIND_Q,))
-            stage3_g(o, KIND_OFF)
             sums_2(e)
 
         def last_half_step():

time: 67.7 us -> 67.5 us (level)
  no operation moved by 1% of the time
where the time goes in v7:
time: 67.5 us; the launch traced here: 67.4 us
  Pallas kernels  67.4 us (100%)
    pallas_call x1, Pallas kernels, call(): pl.pallas_call(kernel, out_shape=(pltpu.VMEM(particles.shape, F32), pltpu...  61.5 us
    pallas_call x1, Pallas kernels, call(): pl.pallas_call(last_kernel, out_shape=jax.ShapeDtypeStruct(particles.shap...  5.96 us

profile of v7, /device:TPU:0, one launch (start us, length us, event | category | flops | bytes accessed | tf_op | source)
XLA Modules:
  0.0 67.4 jit_solution(15632440367684476217)
XLA Ops:
  0.0 61.5 %shard_map.46 = (f32[2,512,4096]{2,1,0:T(8,128)S(1)}, bf16[512,4096]{1,0:T(8,128)(2,1)S(1)}, bf16[512,512]{1,0:T(8,128)(2,1)S(1)}, f32[512,128]{1,0:T(8,128)S(1)}) custom-call(f32[2,512,4096]{2,1,0:T(8,128)} %th_hbm.1, f32[2,4096]{1,0:T(2,128)} %mu_hbm.1, f32[1,4096]{1,0:T(1,128)} %bitcast.1, bf16[4096,128]{1,0:T(8,128)(2,1)} %u_hbm.1), custom_call_target="tpu_custom_call" | custom-call | flops 30000001024 | bytes 18874368 | tf_op jit(solution)/shard_map/pallas_call | solution.py:502
  61.5 6.0 %shard_map.47 = f32[2,512,4096]{2,1,0:T(8,128)} custom-call(f32[2,512,4096]{2,1,0:T(8,128)S(1)} %get-tuple-element.9.theta, bf16[512,4096]{1,0:T(8,128)(2,1)S(1)} %get-tuple-element.10.ybuf, bf16[512,512]{1,0:T(8,128)(2,1)S(1)} %get-tuple-element.11.kfull, f32[512,128]{1,0:T(8,128)S(1)} %get-tuple-element.12.scol), custom_call_target="tpu_custom_call" | custom-call | flops 2000000000 | bytes 16777216 | tf_op jit(solution)/shard_map/pallas_call | solution.py:513
